TPU v7x, 8 devices: a whole 2x2x1 slice. The times are simulated.
8 devices in a mesh: data: 1 (over z), seq: 8 (over y, x, core).
Axes of the slice: x: 2, y: 2, z: 1, core: 2. Of those that a mesh axis runs over, the one named last changes fastest.
Arguments:
- x_tok: bfloat16 [16384, 1280], P(('data', 'seq'))
- dy_tok: bfloat16 [16384, 1280], P(('data', 'seq'))
- ln_gamma: float32 [1280], replicated
- ln_beta: float32 [1280], replicated
- w_qkv: bfloat16 [1280, 3, 16, 80], replicated
- w_out: bfloat16 [1280, 1280], replicated
Outputs:
- output 1: bfloat16 [16384, 1280], P(('data', 'seq'))
- output 2: bfloat16 [16384, 1280], P(('data', 'seq'))
- output 3: float32 [1280, 3, 16, 80], P(('data', 'seq'))
- output 4: float32 [1280, 1280], P(('data', 'seq'))
- output 5: float32 [1280], P('data')
- output 6: float32 [1280], P('data')
All inputs are finite; a program needn't handle non-finite values.
Results may differ from a plain program's by a relative error of at most 0.00435681.
Values are sent between devices in bfloat16 or wider.
A program may use at most 1 GiB of HBM per device.

v0:
```python
import jax
import jax.numpy as jnp
from jax import lax
from jax.sharding import PartitionSpec as P

LN_EPS = 1e-5


def phi_act(t):
    return jnp.where(t > 0, t + 1.0, jnp.exp(jnp.minimum(t, 0.0)))


def phi_slope(t):
    return jnp.where(t > 0, 1.0, jnp.exp(jnp.minimum(t, 0.0)))


def local_block(x_tok, dy_tok, ln_gamma, ln_beta, w_qkv, w_out):
    tokens, width = x_tok.shape
    heads = w_qkv.shape[2]
    head_dim = w_qkv.shape[3]
    x_f32 = x_tok.astype(jnp.float32)
    centered = x_f32 - jnp.mean(x_f32, axis=-1, keepdims=True)
    inv_std = lax.rsqrt(jnp.mean(centered * centered, axis=-1, keepdims=True) + LN_EPS)
    x_hat = centered * inv_std
    normed = (x_hat * ln_gamma + ln_beta).astype(jnp.bfloat16)
    w_flat = w_qkv.reshape(width, 3 * width)
    qkv_all = jnp.dot(normed, w_flat, preferred_element_type=jnp.float32).astype(jnp.bfloat16)
    qkv_all = qkv_all.reshape(tokens, 3, heads, head_dim)
    q_raw = qkv_all[:, 0].astype(jnp.float32)
    k_raw = qkv_all[:, 1].astype(jnp.float32)
    values = qkv_all[:, 2]
    feat_q = phi_act(q_raw).astype(jnp.bfloat16)
    feat_k = phi_act(k_raw).astype(jnp.bfloat16)
    state_part = jnp.einsum("nhi,nhj->hij", feat_k, values, preferred_element_type=jnp.float32)
    norm_part = jnp.sum(feat_k, axis=0, dtype=jnp.float32)
    state, norm_vec = lax.psum((state_part, norm_part), "seq")
    state_b = state.astype(jnp.bfloat16)
    norm_b = norm_vec.astype(jnp.bfloat16)
    numerator = jnp.einsum("nhi,hij->nhj", feat_q, state_b, preferred_element_type=jnp.float32)
    denominator = jnp.einsum("nhi,hi->nh", feat_q, norm_b, preferred_element_type=jnp.float32)
    att_f32 = numerator / denominator[:, :, None]
    att_out = att_f32.astype(jnp.bfloat16).reshape(tokens, width)
    y_tok = (x_f32 + jnp.dot(att_out, w_out, preferred_element_type=jnp.float32)).astype(jnp.bfloat16)
    dwout_part = jnp.einsum("nc,nd->cd", att_out, dy_tok, preferred_element_type=jnp.float32)
    dw_out = lax.psum_scatter(dwout_part, "seq", scatter_dimension=0, tiled=True)
    d_att = jnp.einsum("nd,cd->nc", dy_tok, w_out, preferred_element_type=jnp.float32).reshape(tokens, heads, head_dim)
    g_scaled = (d_att / denominator[:, :, None]).astype(jnp.bfloat16)
    correction = jnp.sum(g_scaled * att_f32, axis=-1)
    d_fq = jnp.einsum("nhj,hij->nhi", g_scaled, state_b, preferred_element_type=jnp.float32) - correction[:, :, None] * norm_b
    dstate_part = jnp.einsum("nhi,nhj->hij", feat_q, g_scaled, preferred_element_type=jnp.float32)
    dnorm_part = -jnp.sum(correction[:, :, None] * feat_q, axis=0)
    d_state, d_norm = lax.psum((dstate_part, dnorm_part), "seq")
    d_state_b = d_state.astype(jnp.bfloat16)
    d_fk = jnp.einsum("nhj,hij->nhi", values, d_state_b, preferred_element_type=jnp.float32) + d_norm
    d_val = jnp.einsum("nhi,hij->nhj", feat_k, d_state_b, preferred_element_type=jnp.float32)
    d_q = (d_fq * phi_slope(q_raw)).astype(jnp.bfloat16)
    d_k = (d_fk * phi_slope(k_raw)).astype(jnp.bfloat16)
    d_qkv = jnp.stack([d_q, d_k, d_val.astype(jnp.bfloat16)], axis=1).reshape(tokens, 3 * width)
    dwqkv_part = jnp.einsum("nc,nf->cf", normed, d_qkv, preferred_element_type=jnp.float32).reshape(width, 3, heads, head_dim)
    dw_qkv = lax.psum_scatter(dwqkv_part, "seq", scatter_dimension=0, tiled=True)
    d_normed = jnp.einsum("nf,cf->nc", d_qkv, w_flat, preferred_element_type=jnp.float32)
    d_gamma, d_beta = lax.psum((jnp.sum(d_normed * x_hat, axis=0), jnp.sum(d_normed, axis=0)), "seq")
    scaled_grad = d_normed * ln_gamma
    d_ln = inv_std * (scaled_grad - jnp.mean(scaled_grad, axis=-1, keepdims=True) - x_hat * jnp.mean(scaled_grad * x_hat, axis=-1, keepdims=True))
    dx_tok = (dy_tok.astype(jnp.float32) + d_ln).astype(jnp.bfloat16)
    return y_tok, dx_tok, dw_qkv, dw_out, d_gamma, d_beta


def solution(mesh):
    rows = P(("data", "seq"), None)
    return jax.shard_map(
        local_block, mesh=mesh,
        in_specs=(rows, rows, P(None), P(None), P(None, None, None, None), P(None, None)),
        out_specs=(rows, rows, P(("data", "seq"), None, None, None), rows, P("data"), P("data")),
        check_vma=False)
```

profile of v0, /device:TPU:0, one launch (start us, length us, event | category | flops | bytes accessed | tf_op | source)
XLA Modules:
  0.0 492.0 jit_solution(554920522191600446)
XLA Ops:
  10.7 4.1 fusion.16
  18.9 28.4 %convolution_convert_fusion = bf16[2048,3840]{1,0:T(8,128)(2,1)} fusion(bf16[1280,3840]{0,1:T(8,128)(2,1)} %bitcast.128, bf16[2048,1280]{1,0:T(8,128)(2,1)S(1)} %copy-done.1, f32[1280]{0:T(1024)S(1)} %copy-done.8, f32[1280]{0:T(1024)S(1)} %copy-done.6, f32[2048]{0:T(1024)S(1)} %add_rsqrt_fusion, f32[2048]{0:T(1024)S(1)} %broadcast_multiply_fusion.2), kind=kOutput, calls=%fused_computation.12 | convolution fusion | flops 20156252160 | bytes 30828544 | tf_op jit(solution)/shard_map/dot_general | solution.py:27
  47.2 20.9 %copy.19 = bf16[2048,3840]{0,1:T(8,128)(2,1)} copy(bf16[2048,3840]{1,0:T(8,128)(2,1)} %convolution_convert_fusion) | data formatting | bytes 31457280 | tf_op jit(solution)/shard_map/convert_element_type | solution.py:27
  68.2 5.3 %convert_reduce_fusion.1 = f32[16,80]{1,0:T(8,128)S(1)} fusion(bf16[2048,3,16,80]{0,3,2,1:T(8,128)(2,1)} %bitcast.111), kind=kLoop, calls=%fused_computation.50 | loop fusion | flops 20970240 | bytes 5248000 | tf_op jit(solution)/shard_map/reduce_sum | solution.py:35
  73.4 7.7 %fusion.39 = f32[16,80,80]{2,1,0:T(8,128)} fusion(bf16[2048,3,16,80]{0,3,2,1:T(8,128)(2,1)} %bitcast.112), kind=kOutput, calls=%fused_computation.60 | convolution fusion | flops 435159040 | bytes 10895360 | tf_op jit(solution)/shard_map/nhi,nhj->hij/dot_general | solution.py:34
  81.2 30.9 %all-reduce.5 = (bf16[16,80]{1,0:T(8,128)(2,1)S(1)}, bf16[16,80,80]{2,1,0:T(8,128)(2,1)}) all-reduce(f32[16,80]{1,0:T(8,128)S(1)} %convert_reduce_fusion.1, f32[16,80,80]{2,1,0:T(8,128)} %fusion.39), channel_id=1, replica_groups=mesh['data'=1,'seq'=8] {'seq'}, use_global_device_ids=true, to_apply=%region_4.5 | all-reduce | flops 103680 | bytes 622080 | tf_op jit(solution)/shard_map/psum | solution.py:36
  112.1 5.3 %fusion.44 = f32[16,1,2048]{2,1,0:T(1,128)S(1)} fusion(bf16[16,80,1]{1,0,2:T(8,128)(2,1)S(1)} %bitcast.127, bf16[2048,3,16,80]{0,3,2,1:T(8,128)(2,1)} %bitcast.113), kind=kOutput, calls=%fused_computation.66 | convolution fusion | flops 20971520 | bytes 5376512 | tf_op jit(solution)/shard_map/nhi,hi->nh/dot_general | solution.py:40
  117.5 9.5 %fusion.56 = f32[2048,1280]{0,1:T(8,128)} fusion(bf16[2048,1280]{1,0:T(8,128)(2,1)S(1)} %bitcast.125, bf16[1280,1280]{1,0:T(8,128)(2,1)S(1)} %copy-done), kind=kOutput, calls=%fused_computation.77 | convolution fusion | flops 6710886400 | bytes 19005440 | tf_op jit(solution)/shard_map/nd,cd->nc/dot_general | solution.py:46
  127.0 10.4 %multiply_reduce_fusion.1 = (f32[2048,16]{0,1:T(8,128)S(1)}, bf16[2048,16,80]{0,2,1:T(8,128)(2,1)}, bf16[2048,16,80]{0,2,1:T(8,128)(2,1)}) fusion(f32[2048,16,80]{0,2,1:T(8,128)} %bitcast.129, f32[2048,16]{0,1:T(8,128)S(1)} %bitcast.126, bf16[16,80,80]{2,1,0:T(8,128)(2,1)} %get-tuple-element.27, bf16[2048,3,16,80]{0,3,2,1:T(8,128)(2,1)S(1)} %bitcast.118), kind=kOutput, calls=%fused_computation.48 | convolution fusion | flops 453476352 | bytes 26681344 | tf_op jit(solution)/shard_map/nhi,hij->nhj/dot_general | solution.py:39
  137.4 11.2 %multiply_reduce_fusion = f32[16,80]{1,0:T(8,128)S(1)} fusion(f32[2048,16]{0,1:T(8,128)S(1)} %get-tuple-element.28, bf16[2048,3,16,80]{0,3,2,1:T(8,128)(2,1)S(1)} %bitcast.119), kind=kLoop, calls=%fused_computation.47 | loop fusion | flops 23591680 | bytes 5379072 | tf_op jit(solution)/shard_map/reduce_sum | solution.py:51
  148.7 6.2 %fusion.52 = f32[16,80,80]{2,1,0:T(8,128)} fusion(bf16[2048,16,80]{0,2,1:T(8,128)(2,1)} %get-tuple-element.29, bf16[2048,3,16,80]{0,3,2,1:T(8,128)(2,1)S(1)} %bitcast.120), kind=kOutput, calls=%fused_computation.76 | convolution fusion | flops 435159040 | bytes 10895360 | tf_op jit(solution)/shard_map/nhi,nhj->hij/dot_general | solution.py:50
  154.9 9.1 %fusion.34 = bf16[2048,1,16,80]{0,3,2,1:T(8,128)(2,1)} fusion(f32[16,80]{1,0:T(8,128)S(1)} %convert_element_type.221, f32[2048,16]{0,1:T(8,128)S(1)} %get-tuple-element.28, bf16[2048,16,80]{0,2,1:T(8,128)(2,1)} %get-tuple-element.29, bf16[2048,3,16,80]{0,3,2,1:T(8,128)(2,1)S(1)} %bitcast.121, bf16[16,80,80]{2,1,0:T(8,128)(2,1)S(1)} %copy-done.9), kind=kOutput, calls=%fused_computation.53 | convolution fusion | flops 440401920 | bytes 16069632 | tf_op jit(solution)/shard_map/nhj,hij->nhi/dot_general | solution.py:49
  164.0 28.6 %all-reduce.6 = (bf16[16,80,80]{2,1,0:T(8,128)(2,1)}, f32[16,80]{1,0:T(8,128)S(1)}) all-reduce(f32[16,80,80]{2,1,0:T(8,128)} %fusion.52, f32[16,80]{1,0:T(8,128)S(1)} %neg.3), channel_id=1, replica_groups=mesh['data'=1,'seq'=8] {'seq'}, use_global_device_ids=true, to_apply=%region_6.7 | all-reduce | flops 103680 | bytes 624640 | tf_op jit(solution)/shard_map/psum | solution.py:52
  192.6 6.2 %convert_bitcast_fusion = bf16[2048,1,16,80]{0,3,2,1:T(8,128)(2,1)S(1)} fusion(bf16[16,80,80]{2,1,0:T(8,128)(2,1)} %get-tuple-element.24, bf16[2048,3,16,80]{0,3,2,1:T(8,128)(2,1)} %bitcast.114), kind=kOutput, calls=%fused_computation.59 | convolution fusion | flops 437780480 | bytes 10813440 | tf_op jit(solution)/shard_map/nhi,hij->nhj/dot_general | solution.py:55
  198.9 11.4 %fusion.36 = bf16[2048,1,16,80]{0,3,2,1:T(8,128)(2,1)} fusion(f32[16,80]{1,0:T(8,128)S(1)} %get-tuple-element.25, bf16[2048,3,16,80]{0,3,2,1:T(8,128)(2,1)} %bitcast.115, bf16[16,80,80]{2,1,0:T(8,128)(2,1)S(1)} %copy-done.10), kind=kOutput, calls=%fused_computation.55 | convolution fusion | flops 437780480 | bytes 15938560 | tf_op jit(solution)/shard_map/nhj,hij->nhi/dot_general | solution.py:54
  210.3 38.9 %fusion = f32[1280,3,16,80]{3,0,2,1:T(8,128)} fusion(bf16[2048,1,16,80]{0,3,2,1:T(8,128)(2,1)S(1)} %convert_bitcast_fusion, bf16[2048,1,16,80]{0,3,2,1:T(8,128)(2,1)} %fusion.36, bf16[2048,1,16,80]{0,3,2,1:T(8,128)(2,1)S(1)} %bitcast.133, bf16[2048,1280,1,1]{1,0,3,2:T(8,128)(2,1)S(1)} %bitcast.123), kind=kOutput, calls=%fused_computation.1 | convolution fusion | flops 20179845120 | bytes 40632320 | tf_op jit(solution)/shard_map/nc,nf->cf/dot_general | solution.py:59
  249.3 12.4 %fusion.57 = f32[1280,1280]{1,0:T(8,128)} fusion(bf16[2048,1280]{0,1:T(8,128)(2,1)} %bitcast.130, bf16[2048,1280]{1,0:T(8,128)(2,1)} %param.7), kind=kOutput, calls=%fused_computation.78 | convolution fusion | flops 6710886400 | bytes 17039360 | tf_op jit(solution)/shard_map/nc,nd->cd/dot_general | solution.py:44
  261.8 31.9 %fusion.15 = (f32[1280]{0:T(1024)S(1)}, f32[2048]{0:T(1024)S(1)}, f32[2048]{0:T(1024)S(1)}, f32[1280]{0:T(1024)S(1)}, f32[2048,1280,1,1]{1,0,3,2:T(8,128)}) fusion(bf16[2048,1280]{1,0:T(8,128)(2,1)} %param.6, f32[2048]{0:T(1024)S(1)} %copy-done.5, f32[2048]{0:T(1024)S(1)} %copy-done.3, f32[1280]{0:T(1024)S(1)} %copy-done.7, ...), kind=kOutput, calls=%fused_computation.26 | convolution fusion | flops 20174594048 | bytes 41335808 | tf_op jit(solution)/shard_map/nf,cf->nc/dot_general | solution.py:61
  293.7 23.3 %all-reduce = (f32[1280]{0:T(1024)}, f32[1280]{0:T(1024)}) all-reduce(f32[1280]{0:T(1024)S(1)} %get-tuple-element.18, f32[1280]{0:T(1024)S(1)} %get-tuple-element.21), channel_id=1, replica_groups=mesh['data'=1,'seq'=8] {'seq'}, use_global_device_ids=true, to_apply=%region_14.15 | all-reduce | flops 2560 | bytes 20480 | tf_op jit(solution)/shard_map/psum | solution.py:62
  317.0 11.4 %fusion.14 = bf16[2048,1280]{1,0:T(8,128)(2,1)} fusion(bf16[2048,1280]{1,0:T(8,128)(2,1)} %param.6, bf16[2048,1280]{1,0:T(8,128)(2,1)} %param.7, f32[2048,1280,1,1]{1,0,3,2:T(8,128)} %get-tuple-element.32, f32[2048]{0:T(1024)S(1)} %get-tuple-element.33, f32[2048]{0:T(1024)S(1)} %get-tuple-element.34, f32[1280]{0:T(1024)S(1)} %copy-done.7, ...), kind=kLoop, calls=%fused_computation.25 | loop fusion | flops 28835840 | bytes 26252288 | tf_op jit(solution)/shard_map/convert_element_type | solution.py:65
  328.4 11.3 %fusion.17 = bf16[2048,1280]{1,0:T(8,128)(2,1)} fusion(bf16[2048,1280]{1,0:T(8,128)(2,1)} %param.6, bf16[2048,1280]{0,1:T(8,128)(2,1)} %bitcast.131, bf16[1280,1280]{1,0:T(8,128)(2,1)S(1)} %copy-done), kind=kOutput, calls=%fused_computation.28 | convolution fusion | flops 6718750720 | bytes 19005440 | tf_op jit(solution)/shard_map/dot_general | solution.py:43
  339.7 87.0 %reduce-scatter.3.cloned.1.call-done = f32[160,3,16,80]{3,0,2,1:T(8,128)} async-done(((f32[1280,3,16,80]{3,0,2,1:T(8,128)}), f32[160,3,16,80]{3,0,2,1:T(8,128)}) %reduce-scatter.3.cloned.1.call-update) | async-done | bytes 2457616 | tf_op jit(solution)/shard_map/reduce_scatter | solution.py:60
  426.7 6.3 %copy.23 = f32[160,3,16,80]{3,2,1,0:T(8,128)} copy(f32[160,3,16,80]{3,0,2,1:T(8,128)} %reduce-scatter.3.cloned.1.call-done) | data formatting | bytes 4915200
  433.0 51.6 %reduce-scatter.5.cloned.1.call-done = f32[160,1280]{1,0:T(8,128)} async-done(((f32[1280,1280]{1,0:T(8,128)}), f32[160,1280]{1,0:T(8,128)}) %reduce-scatter.5.cloned.1.call-update) | async-done | bytes 819216 | tf_op jit(solution)/shard_map/reduce_scatter | solution.py:45
  (60 shorter events, 7.7 us)
Async XLA Ops:
  7.2 110.3 %copy-start = (bf16[1280,1280]{1,0:T(8,128)(2,1)S(1)}, bf16[1280,1280]{1,0:T(8,128)(2,1)}, u32[]{:S(2)}) copy-start(bf16[1280,1280]{1,0:T(8,128)(2,1)} %param.11) | copy-start | bytes 9830404
  7.2 7.7 %copy-start.6 = (f32[1280]{0:T(1024)S(1)}, f32[1280]{0:T(1024)}, u32[]{:S(2)}) copy-start(f32[1280]{0:T(1024)} %param.8) | copy-start | bytes 15364
  7.2 7.7 %copy-start.8 = (f32[1280]{0:T(1024)S(1)}, f32[1280]{0:T(1024)}, u32[]{:S(2)}) copy-start(f32[1280]{0:T(1024)} %param.9) | copy-start | bytes 15364
  7.2 419.5 %reduce-scatter.3.cloned.1.call-start = ((), (), s32[]{:S(2)}) async-start(), calls=%async_computation.2 | async-start | bytes 35389440 | tf_op jit(solution)/shard_map/reduce_scatter | solution.py:60
  7.2 7.6 %copy-start.1 = (bf16[2048,1280]{1,0:T(8,128)(2,1)S(1)}, bf16[2048,1280]{1,0:T(8,128)(2,1)}, u32[]{:S(2)}) copy-start(bf16[2048,1280]{1,0:T(8,128)(2,1)} %param.6) | copy-start | bytes 15728644
  10.7 8.2 %copy-start.2 = (f32[2048]{0:T(1024)}, f32[2048]{0:T(1024)S(1)}, u32[]{:S(2)}) copy-start(f32[2048]{0:T(1024)S(1)} %broadcast_multiply_fusion.2) | copy-start | bytes 24580
  14.9 4.0 copy-start.4
  112.1 5.4 %slice-start.6 = ((s8[5242880]{0:T(1024)(128)(4,1)}), s8[4194304]{0:T(1024)(128)(4,1)S(1)}, s32[]{:S(2)}) async-start(s8[5242880]{0:T(1024)(128)(4,1)} %bitcast.124), calls=%async_computation.10 | async-start | bytes 8388608
  112.1 5.4 %slice-start.7 = ((s8[5242880]{0:T(1024)(128)(4,1)}), s8[1048576]{0:T(1024)(128)(4,1)S(1)}, s32[]{:S(2)}) async-start(s8[5242880]{0:T(1024)(128)(4,1)} %bitcast.124), calls=%async_computation.11 | async-start | bytes 2097152
  112.1 14.9 %slice-start = ((s8[15728640]{0:T(1024)(128)(4,1)}), s8[4194304]{0:T(1024)(128)(4,1)S(1)}, s32[]{:S(2)}) async-start(s8[15728640]{0:T(1024)(128)(4,1)} %bitcast.116), calls=%async_computation.4 | async-start | bytes 8388608
  112.1 14.9 %slice-start.1 = ((s8[15728640]{0:T(1024)(128)(4,1)}), s8[4194304]{0:T(1024)(128)(4,1)S(1)}, s32[]{:S(2)}) async-start(s8[15728640]{0:T(1024)(128)(4,1)} %bitcast.116), calls=%async_computation.5 | async-start | bytes 8388608
  117.5 9.5 %slice-start.2 = ((s8[15728640]{0:T(1024)(128)(4,1)}), s8[4194304]{0:T(1024)(128)(4,1)S(1)}, s32[]{:S(2)}) async-start(s8[15728640]{0:T(1024)(128)(4,1)} %bitcast.116), calls=%async_computation.6 | async-start | bytes 8388608
  117.5 9.5 %slice-start.3 = ((s8[15728640]{0:T(1024)(128)(4,1)}), s8[3145728]{0:T(1024)(128)(4,1)S(1)}, s32[]{:S(2)}) async-start(s8[15728640]{0:T(1024)(128)(4,1)} %bitcast.116), calls=%async_computation.7 | async-start | bytes 6291456
  148.6 6.2 %copy-start.9 = (bf16[16,80,80]{2,1,0:T(8,128)(2,1)S(1)}, bf16[16,80,80]{2,1,0:T(8,128)(2,1)}, u32[]{:S(2)}) copy-start(bf16[16,80,80]{2,1,0:T(8,128)(2,1)} %get-tuple-element.27) | copy-start | bytes 614404
  192.6 6.3 %copy-start.10 = (bf16[16,80,80]{2,1,0:T(8,128)(2,1)S(1)}, bf16[16,80,80]{2,1,0:T(8,128)(2,1)}, u32[]{:S(2)}) copy-start(bf16[16,80,80]{2,1,0:T(8,128)(2,1)} %get-tuple-element.24) | copy-start | bytes 614404
  192.6 17.7 %slice-start.4 = ((s8[5242880]{0:T(1024)(128)(4,1)}), s8[4194304]{0:T(1024)(128)(4,1)S(1)}, s32[]{:S(2)}) async-start(s8[5242880]{0:T(1024)(128)(4,1)} %bitcast.122), calls=%async_computation.8 | async-start | bytes 8388608
  192.6 17.7 %slice-start.8 = ((s8[5242880]{0:T(1024)(128)(4,1)}), s8[4194304]{0:T(1024)(128)(4,1)S(1)}, s32[]{:S(2)}) async-start(s8[5242880]{0:T(1024)(128)(4,1)} %bitcast.132), calls=%async_computation.12 | async-start | bytes 8388608
  198.8 11.4 %copy-start.11 = (bf16[2048,1,16,80]{0,3,2,1:T(8,128)(2,1)}, bf16[2048,1,16,80]{0,3,2,1:T(8,128)(2,1)S(1)}, u32[]{:S(2)}) copy-start(bf16[2048,1,16,80]{0,3,2,1:T(8,128)(2,1)S(1)} %convert_bitcast_fusion) | copy-start | bytes 15728644
  198.8 11.4 %slice-start.5 = ((s8[5242880]{0:T(1024)(128)(4,1)}), s8[1048576]{0:T(1024)(128)(4,1)S(1)}, s32[]{:S(2)}) async-start(s8[5242880]{0:T(1024)(128)(4,1)} %bitcast.122), calls=%async_computation.9 | async-start | bytes 2097152
  198.8 11.4 %slice-start.9 = ((s8[5242880]{0:T(1024)(128)(4,1)}), s8[1048576]{0:T(1024)(128)(4,1)S(1)}, s32[]{:S(2)}) async-start(s8[5242880]{0:T(1024)(128)(4,1)} %bitcast.132), calls=%async_computation.13 | async-start | bytes 2097152
  249.2 235.5 %reduce-scatter.5.cloned.1.call-start = ((), (), s32[]{:S(2)}) async-start(), calls=%async_computation.3 | async-start | bytes 7372800 | tf_op jit(solution)/shard_map/reduce_scatter | solution.py:45
  249.2 12.5 %copy-start.3 = (f32[2048]{0:T(1024)S(1)}, f32[2048]{0:T(1024)}, u32[]{:S(2)}) copy-start(f32[2048]{0:T(1024)} %copy-done.2) | copy-start | bytes 24580
  249.3 12.5 %copy-start.5 = (f32[2048]{0:T(1024)S(1)}, f32[2048]{0:T(1024)}, u32[]{:S(2)}) copy-start(f32[2048]{0:T(1024)} %copy-done.4) | copy-start | bytes 24580
  249.3 12.5 %copy-start.7 = (f32[1280]{0:T(1024)S(1)}, f32[1280]{0:T(1024)}, u32[]{:S(2)}) copy-start(f32[1280]{0:T(1024)} %param.8) | copy-start | bytes 15364
Sparse Core Ops, SparseCore 0:
  249.3 177.3 reduce-scatter.2
  430.6 53.9 reduce-scatter.4
where the time goes:
time: 501 us; the launch traced here: 492 us
  matrix products  189 us (38%)
  waiting for transfers between devices  139 us (28%)
  blocking collectives  82.8 us (17%)
  other arithmetic  39.5 us (8%)
  local copies, waits for them, and re-layouts  27.4 us (5%)
  between operations  14.9 us (3%)
    reduce_scatter x1, waiting for transfers between devices, local_block(): lax.psum_scatter(dwqkv_part, 'seq', scatter_dimension=0, tiled=True)  87 us
    reduce_scatter x1, waiting for transfers between devices, local_block(): lax.psum_scatter(dwout_part, 'seq', scatter_dimension=0, tiled=True)  51.6 us
    dot_general x1, matrix products, local_block(): jnp.einsum('nc,nf->cf', normed, d_qkv, preferred_element_type=jnp.float32)  38.9 us
    dot_general x1, matrix products, local_block(): jnp.einsum('nf,cf->nc', d_qkv, w_flat, preferred_element_type=jnp.float32)  31.9 us
    psum x1, blocking collectives, local_block(): state, norm_vec = lax.psum((state_part, norm_part), 'seq')  30.9 us
    psum x1, blocking collectives, local_block(): d_state, d_norm = lax.psum((dstate_part, dnorm_part), 'seq')  28.6 us
    dot_general x1, matrix products, local_block(): jnp.dot(normed, w_flat, preferred_element_type=jnp.float32)  28.4 us
    psum x1, blocking collectives, local_block(): lax.psum((jnp.sum(d_normed * x_hat, axis=0), jnp.sum(d_normed, axis=0)),...  23.3 us
  transfers between devices with their start and end apart: 2, of which 2 were waited for; matrix products, arithmetic and copies ran while one was open for 15% of the time, Pallas kernels for 0%

commit v1 on v0

v1 whole, which is shorter than its diff:
```python
import functools

import jax
import jax.numpy as jnp
from jax import lax
from jax.experimental import pallas as pl
from jax.experimental.pallas import tpu as pltpu
from jax.sharding import PartitionSpec as P

LN_EPS = 1e-5
T = 2048
D = 1280
HD = 80
NH = 16
R = 256
NT_ = T // R
C = 256
NJ = D // C
BW = 512
BAND = [min(max(C * j - 128, 0), D - BW) for j in range(NJ)]
PIECE = D // 8
NCH = 4 * NJ
SLOTS = 8
LAG = 4
f32 = jnp.float32
bf16 = jnp.bfloat16


def dot_nn(a, b):
    return lax.dot_general(a, b, (((1,), (0,)), ((), ())), preferred_element_type=f32)


def dot_nt(a, b):
    return lax.dot_general(a, b, (((1,), (1,)), ((), ())), preferred_element_type=f32)


def dot_tn(a, b):
    return lax.dot_general(a, b, (((0,), (0,)), ((), ())), preferred_element_type=f32)


def phi(t):
    return jnp.where(t > 0, t + 1.0, jnp.exp(jnp.minimum(t, 0.0)))


def slope(t):
    return jnp.where(t > 0, 1.0, jnp.exp(jnp.minimum(t, 0.0)))


def head_of(idx):
    return (idx * 6554) >> 19


def normalise(x):
    centered = x - jnp.mean(x, axis=-1, keepdims=True)
    inv = lax.rsqrt(jnp.mean(centered * centered, axis=-1, keepdims=True) + LN_EPS)
    return centered * inv, inv


def block(x, dy, w_t, w_o, gam, bet,
          y, dx, dw, dgb,
          u_s, g_s, o_s, qkv_s, wo_s, bd_s, zb_s, on_s, tile_s,
          f_s, acc_s, ph_s, pl_s, c_s, st_s, part_s, rsr_s, ag_s, gbr_s, gb_s,
          p_s, r1_s, ra_s, rb_s, ra2_s, rb2_s, ost_s,
          xsem, dsem, ysem, wsem, lsem, osem, ar_send, ar_recv, gb_send, gb_recv,
          dd_send, dd_recv, ln_send, ln_recv):
    s = lax.axis_index("seq")
    core = s % 2
    px = (s // 2) % 2
    py = s // 4
    mate = s + 1 - 2 * core
    xnb = s + 2 - 4 * px
    ynb = s + 4 - 8 * py

    def remote(src, dst, ssem, rsem, dev):
        return pltpu.make_async_remote_copy(src_ref=src, dst_ref=dst, send_sem=ssem, recv_sem=rsem,
                                            device_id={"seq": dev}, device_id_type=pl.DeviceIdType.MESH)

    def rows(t):
        return pl.ds(pl.multiple_of(t * R, R), R)

    def cols(j):
        return pl.ds(pl.multiple_of(j * C, C), C)

    def x_in(t):
        return pltpu.make_async_copy(x.at[rows(t), :], tile_s.at[t % 2], xsem.at[t % 2])

    def dy_in(t):
        return pltpu.make_async_copy(dy.at[rows(t), :], tile_s.at[2 + t % 2], dsem.at[t % 2])

    def tile_out(dst, t):
        return pltpu.make_async_copy(tile_s.at[4 + t % 2], dst.at[rows(t), :], ysem.at[t % 2])

    def w_in(n):
        r = pl.multiple_of(((n + NJ) % (3 * NJ)) * C, C)
        return pltpu.make_async_copy(w_t.at[pl.ds(r, C), :], tile_s.at[2 + n % 3], wsem.at[n % 3])

    dy_all = pltpu.make_async_copy(dy, g_s, lsem.at[0])
    wo_all = pltpu.make_async_copy(w_o, wo_s, lsem.at[1])
    wt_lo = pltpu.make_async_copy(w_t.at[pl.ds(0, T), :], o_s, lsem.at[2])
    wt_hi = pltpu.make_async_copy(w_t.at[pl.ds(T, 3 * D - T), :], g_s.at[pl.ds(0, 3 * D - T), :], lsem.at[0])

    x_in(0).start()
    w_in(0).start()
    w_in(1).start()
    dy_all.start()
    wo_all.start()

    barrier = pltpu.get_barrier_semaphore()
    for k in range(1, 8):
        pl.semaphore_signal(barrier, inc=1, device_id={"seq": (s + k) % 8}, device_id_type=pl.DeviceIdType.MESH)
    pl.semaphore_wait(barrier, 7)

    def pack(a):
        for m in range(110):
            r0, c0 = 8 * (m // 10), 128 * (m % 10)
            part_s[a, m // 14, m % 14] = c_s[r0:r0 + 8, c0:c0 + 128]
        for m in range(110, 112):
            part_s[a, m // 14, m % 14] = jnp.zeros((8, 128), f32)

    def ar_copy(a, phase, k):
        tgt = (s + k) % 8
        if phase == 0:
            return remote(part_s.at[a, tgt], rsr_s.at[a, s], ar_send.at[a, 0, k], ar_recv.at[a, 0, k], tgt)
        return remote(ag_s.at[a, s], ag_s.at[a, s], ar_send.at[a, 1, k], ar_recv.at[a, 1, k], tgt)

    def ar_land(a, phase, k):
        src = (s + 8 - k) % 8
        if phase == 0:
            return remote(part_s.at[a, src], rsr_s.at[a, src], ar_send.at[a, 0, k], ar_recv.at[a, 0, k], src)
        return remote(ag_s.at[a, src], ag_s.at[a, src], ar_send.at[a, 1, k], ar_recv.at[a, 1, k], src)

    def ar_start(a):
        pack(a)
        for k in range(1, 8):
            ar_copy(a, 0, k).start()

    def ar_mid(a):
        total = part_s[a, s]
        for k in range(1, 8):
            ar_land(a, 0, k).wait_recv()
            total = total + rsr_s[a, (s + 8 - k) % 8]
        ag_s[a, s] = total
        for k in range(1, 8):
            ar_copy(a, 1, k).start()

    def ar_end(a):
        for k in range(1, 8):
            ar_land(a, 1, k).wait_recv()
        for k in range(1, 8):
            ar_copy(a, 0, k).wait_send()
            ar_copy(a, 1, k).wait_send()
        for m in range(110):
            r0, c0 = 8 * (m // 10), 128 * (m % 10)
            c_s[r0:r0 + 8, c0:c0 + 128] = ag_s[a, m // 14, m % 14]

    def compact(ref, base, j):
        head = head_of(lax.broadcasted_iota(jnp.int32, (HD, C), 1) + C * j)
        out = jnp.zeros((HD, C), f32)
        for h in range(C * j // HD, (C * j + C - 1) // HD + 1):
            r0 = base + HD * h - BAND[j]
            out = jnp.where(head == h, ref[r0:r0 + HD, :], out)
        c_s[0:HD, C * j:C * j + C] = out

    def expand():
        for h in range(NH):
            c0 = HD * h // 128 * 128
            c1 = -(-(HD * h + HD) // 128) * 128
            head = head_of(lax.broadcasted_iota(jnp.int32, (HD, c1 - c0), 1) + c0)
            bd_s[HD * h:HD * h + HD, c0:c1] = jnp.where(head == h, c_s[0:HD, c0:c1], 0.0).astype(bf16)

    def product(i, lhs, rhs):
        p_s[pl.ds(pl.multiple_of((i % 2) * D, D), D), :] = dot_tn(lhs[...], rhs)

    def dd(i, k):
        src = p_s.at[pl.ds(pl.multiple_of((i % 2) * D + (2 * k + 1 - core) * PIECE, 8), PIECE), :]
        return remote(src, r1_s.at[i % SLOTS, k], dd_send.at[i % 2, k], dd_recv.at[i % 2, k], mate)

    def to_mate(i):
        for k in range(4):
            dd(i, k).start()

    def chip_sum(i):
        for k in range(4):
            dd(i, k).wait_recv()
            own = pl.ds(pl.multiple_of((i % 2) * D + (2 * k + core) * PIECE, 8), PIECE)
            r1_s[i % SLOTS, k] = r1_s[i % SLOTS, k] + p_s[own, :]
            dd(i, k).wait_send()

    def link(i, n):
        slot, q = i % SLOTS, i % LAG
        if n < 2:
            return remote(r1_s.at[slot, 2 * n + 1 - px, :, 0:128], ra_s.at[q, n], ln_send.at[q, n], ln_recv.at[q, n], xnb)
        if n < 4:
            return remote(r1_s.at[slot, 2 * (1 - py) + n - 2, :, 128:256], rb_s.at[q, n - 2], ln_send.at[q, n], ln_recv.at[q, n], ynb)
        if n == 4:
            return remote(r1_s.at[slot, 2 * (1 - py) + px, :, 0:128], ra2_s.at[q], ln_send.at[q, n], ln_recv.at[q, n], ynb)
        return remote(r1_s.at[slot, 2 * py + 1 - px, :, 128:256], rb2_s.at[q], ln_send.at[q, n], ln_recv.at[q, n], xnb)

    def first_hop(i):
        for n in (0, 2, 1, 3):
            link(i, n).start()

    def second_hop(i):
        slot, q = i % SLOTS, i % LAG
        for n in range(2):
            link(i, n).wait_recv()
            r1_s[slot, 2 * n + px, :, 0:128] = r1_s[slot, 2 * n + px, :, 0:128] + ra_s[q, n]
        for n in range(2):
            link(i, n + 2).wait_recv()
            r1_s[slot, 2 * py + n, :, 128:256] = r1_s[slot, 2 * py + n, :, 128:256] + rb_s[q, n]
        link(i, 4).start()
        link(i, 5).start()

    def piece_out(i):
        return pltpu.make_async_copy(ost_s.at[i % 2], dw.at[:, cols(i)], osem.at[i % 2])

    def last_sum(i):
        slot, q = i % SLOTS, i % LAG

        @pl.when(i >= 2)
        def _():
            piece_out(i - 2).wait()

        link(i, 4).wait_recv()
        ost_s[i % 2, :, 0:128] = r1_s[slot, 2 * py + px, :, 0:128] + ra2_s[q]
        link(i, 5).wait_recv()
        ost_s[i % 2, :, 128:256] = r1_s[slot, 2 * py + px, :, 128:256] + rb2_s[q]
        for n in range(6):
            link(i, n).wait_send()
        piece_out(i).start()

    def pump(m, lo, hi):
        @pl.when((m - 4 >= lo) & (m - 4 < hi))
        def _():
            last_sum(m - 4)

        @pl.when((m - 2 >= lo) & (m - 2 < hi))
        def _():
            second_hop(m - 2)

        @pl.when((m >= lo) & (m < hi))
        def _():
            first_hop(m)

    bd_s[...] = jnp.zeros((D, D), bf16)
    gamma = gam[...]
    beta = bet[...]

    @pl.loop(0, NT_)
    def _(t):
        x_in(t).wait()

        @pl.when(t + 1 < NT_)
        def _():
            x_in(t + 1).start()

        x_hat, _ = normalise(tile_s[t % 2].astype(f32))
        u_s[rows(t), :] = (x_hat * gamma + beta).astype(bf16)

    for j in range(NJ):
        hr = head_of(lax.broadcasted_iota(jnp.int32, (C, BW), 0) + C * j)
        hc = head_of(lax.broadcasted_iota(jnp.int32, (C, BW), 1) + BAND[j])
        on_s[j] = jnp.where(hr == hc, 1.0, 0.0).astype(bf16)

    def project(n, which, keep):
        w_in(n).wait()

        @pl.when(n + 2 < 3 * NJ)
        def _():
            w_in(n + 2).start()

        j = n % NJ

        @pl.loop(0, T // 512)
        def _(b):
            r = pl.ds(pl.multiple_of(b * 512, 512), 512)
            out = dot_nt(u_s[r, :], tile_s[2 + n % 3]).astype(bf16)
            qkv_s[which, r, cols(j)] = out
            if keep:
                feat = phi(out.astype(f32)).astype(bf16)
                o_s[r, cols(j)] = feat
                part = jnp.sum(feat.astype(f32), axis=0, keepdims=True)
                before = jnp.where(b == 0, 0.0, c_s[HD:HD + 1, cols(j)])
                c_s[HD:HD + 1, cols(j)] = before + part

    c_s[HD:HD + 8, :] = jnp.zeros((8, D), f32)

    @pl.loop(0, NJ)
    def _(n):
        project(n, 1, True)

    @pl.loop(NJ, 2 * NJ)
    def _(n):
        project(n, 2, False)

    for j in range(NJ):
        st_s[...] = dot_tn(o_s[:, BAND[j]:BAND[j] + BW], qkv_s[2, :, C * j:C * j + C])
        compact(st_s, 0, j)
    ar_start(0)

    @pl.loop(2 * NJ, 3 * NJ - 1)
    def _(n):
        project(n, 0, False)

    ar_mid(0)
    project(3 * NJ - 1, 0, False)
    ar_end(0)
    expand()
    for j in range(NJ):
        z = c_s[HD:HD + 1, BAND[j]:BAND[j] + BW]
        zb_s[j] = jnp.where(on_s[j].astype(f32) > 0.5, jnp.broadcast_to(z, (C, BW)), 0.0).astype(bf16)

    def num_den(j):
        f = f_s[:, BAND[j]:BAND[j] + BW]
        return dot_nn(f, bd_s[BAND[j]:BAND[j] + BW, C * j:C * j + C]), dot_nt(f, zb_s[j])

    @pl.loop(0, NT_)
    def _(t):
        f_s[...] = phi(qkv_s[0, rows(t), :].astype(f32)).astype(bf16)
        for j in range(NJ):
            num, den = num_den(j)
            o_s[rows(t), C * j:C * j + C] = (num / den).astype(bf16)

    dy_all.wait()
    wo_all.wait()

    @pl.loop(0, NJ)
    def _(i):
        product(i, o_s, g_s[:, cols(i)])

        @pl.when(i > 0)
        def _():
            chip_sum(i - 1)

        to_mate(i)

        @pl.when(i == 1)
        def _():
            pump(0, 0, NJ)

    chip_sum(NJ - 1)
    pump(1, 0, NJ)

    p_s[...] = jnp.zeros((2 * D, C), f32)
    st_s[0:8, 0:C] = jnp.zeros((8, C), f32)
    gb_s[...] = jnp.zeros((8, D), f32)

    @pl.loop(0, NT_)
    def _(t):
        acc_s[...] = dot_nt(g_s[rows(t), :], wo_s[...])
        f_s[...] = phi(qkv_s[0, rows(t), :].astype(f32)).astype(bf16)
        for j in range(NJ):
            cj = slice(C * j, C * j + C)
            num, den = num_den(j)
            g = (acc_s[:, cj] / den).astype(bf16)
            g_s[rows(t), cj] = g
            prod = g.astype(f32) * (num / den)
            high = prod.astype(bf16)
            ph_s[:, cj] = high
            pl_s[:, cj] = (prod - high.astype(f32)).astype(bf16)
        for j in range(NJ):
            cj = slice(C * j, C * j + C)
            band = slice(BAND[j], BAND[j] + BW)
            corr = dot_nt(ph_s[:, band], on_s[j]) + dot_nt(pl_s[:, band], on_s[j])
            d_f = dot_nt(g_s[rows(t), band], bd_s[cj, band]) - corr * c_s[HD:HD + 1, cj].astype(bf16).astype(f32)
            raw = qkv_s[0, rows(t), cj].astype(f32)
            qkv_s[0, rows(t), cj] = (d_f * slope(raw)).astype(bf16)
            gb_s[0:1, cj] = gb_s[0:1, cj] + jnp.sum(corr * f_s[:, cj].astype(f32), axis=0, keepdims=True)
            p_s[BW * j:BW * j + BW, :] = p_s[BW * j:BW * j + BW, :] + dot_tn(f_s[:, band], g_s[rows(t), cj])

        @pl.when(t % 2 == 1)
        def _():
            pump(2 + t // 2, 0, NJ)

    for j in range(NJ):
        compact(p_s, BW * j, j)
    c_s[HD:HD + 1, :] = -gb_s[0:1, :]
    ar_start(1)
    wt_hi.start()

    @pl.loop(6, 9)
    def _(m):
        pump(m, 0, NJ)

    def weight_chunk(i):
        n = i - NJ
        product(i, u_s, qkv_s[n // NJ, :, cols(n % NJ)])

    @pl.loop(NJ, 2 * NJ)
    def _(i):
        weight_chunk(i)

        @pl.when(i > NJ)
        def _():
            chip_sum(i - 1)

        to_mate(i)

        @pl.when((i == NJ + 1) | (i == NJ + 3))
        def _():
            pump(NJ + (i - NJ) // 2, NJ, NCH)

    chip_sum(2 * NJ - 1)
    ar_mid(1)

    x_in(0).start()

    @pl.loop(0, NT_)
    def _(t):
        x_in(t).wait()

        @pl.when(t + 1 < NT_)
        def _():
            x_in(t + 1).start()

        @pl.when(t >= 2)
        def _():
            tile_out(y, t - 2).wait()

        tile_s[4 + t % 2] = (tile_s[t % 2].astype(f32) + dot_nn(o_s[rows(t), :], wo_s[...])).astype(bf16)
        tile_out(y, t).start()

        @pl.when(t % 4 == 3)
        def _():
            pump(NJ + 2 + t // 4, NJ, NCH)

    wt_lo.start()
    tile_out(y, NT_ - 2).wait()
    tile_out(y, NT_ - 1).wait()
    ar_end(1)
    expand()

    @pl.loop(0, NT_)
    def _(t):
        f_s[...] = phi(qkv_s[1, rows(t), :].astype(f32)).astype(bf16)
        ph_s[...] = qkv_s[2, rows(t), :]
        for j in range(NJ):
            cj = slice(C * j, C * j + C)
            band = slice(BAND[j], BAND[j] + BW)
            d_f = dot_nt(ph_s[:, band], bd_s[cj, band]) + c_s[HD:HD + 1, cj]
            raw = qkv_s[1, rows(t), cj].astype(f32)
            qkv_s[1, rows(t), cj] = (d_f * slope(raw)).astype(bf16)
            qkv_s[2, rows(t), cj] = dot_nn(f_s[:, band], bd_s[band, cj]).astype(bf16)

        @pl.when(t == 3)
        def _():
            pump(NJ + 4, NJ, NCH)

    @pl.loop(2 * NJ, 2 * NJ + 2)
    def _(i):
        weight_chunk(i)

        @pl.when(i > 2 * NJ)
        def _():
            chip_sum(i - 1)

        to_mate(i)

    gb_s[...] = jnp.zeros((8, D), f32)
    x_in(0).start()
    dy_in(0).start()
    wt_lo.wait()
    wt_hi.wait()

    @pl.loop(0, NT_)
    def _(t):
        pump(2 * NJ + t, NJ, NCH)
        weight_chunk(2 * NJ + 2 + t)
        chip_sum(2 * NJ + 1 + t)
        to_mate(2 * NJ + 2 + t)
        x_in(t).wait()
        dy_in(t).wait()

        @pl.when(t + 1 < NT_)
        def _():
            x_in(t + 1).start()
            dy_in(t + 1).start()

        @pl.when(t >= 2)
        def _():
            tile_out(dx, t - 2).wait()

        cut = T - D
        for j in range(NJ):
            cj = slice(C * j, C * j + C)
            acc_s[:, cj] = (dot_nn(qkv_s[0, rows(t), :], o_s[0:D, cj])
                            + dot_nn(qkv_s[1, rows(t), 0:cut], o_s[D:T, cj])
                            + dot_nn(qkv_s[1, rows(t), cut:D], g_s[0:D - cut, cj])
                            + dot_nn(qkv_s[2, rows(t), :], g_s[D - cut:2 * D - cut, cj]))
        du = acc_s[...]
        x_hat, inv = normalise(tile_s[t % 2].astype(f32))
        dux = du * x_hat
        gb_s[0:1, :] = gb_s[0:1, :] + jnp.sum(dux, axis=0, keepdims=True)
        gb_s[1:2, :] = gb_s[1:2, :] + jnp.sum(du, axis=0, keepdims=True)
        e = du * gamma
        m1 = jnp.mean(e, axis=-1, keepdims=True)
        m2 = jnp.mean(e * x_hat, axis=-1, keepdims=True)
        tile_s[4 + t % 2] = (tile_s[2 + t % 2].astype(f32) + inv * (e - m1 - x_hat * m2)).astype(bf16)
        tile_out(dx, t).start()

    def gb_copy(k):
        return remote(gb_s, gbr_s.at[k], gb_send.at[k], gb_recv.at[k], (s + k) % 8)

    for k in range(1, 8):
        gb_copy(k).start()
    pump(NCH - 2, NJ, NCH)
    chip_sum(NCH - 1)

    @pl.loop(NCH - 1, NCH + 4)
    def _(m):
        pump(m, NJ, NCH)

    tile_out(dx, NT_ - 2).wait()
    tile_out(dx, NT_ - 1).wait()
    for k in range(1, 8):
        gb_copy(k).wait_recv()
        gb_copy(k).wait_send()
    gbr_s[0] = gb_s[...]
    total = jnp.zeros((8, D), f32)
    for d in range(8):
        total = total + gbr_s[(s + 8 - d) % 8]
    dgb[...] = total
    piece_out(NCH - 2).wait()
    piece_out(NCH - 1).wait()


def local_block(x_tok, dy_tok, ln_gamma, ln_beta, w_qkv, w_out):
    w_t = jnp.transpose(w_qkv, (1, 2, 3, 0)).reshape(3 * D, D)
    hbm = pl.BlockSpec(memory_space=pl.ANY)
    vmem = pl.BlockSpec(memory_space=pltpu.VMEM)
    dma = pltpu.SemaphoreType.DMA
    scratch = [
        pltpu.VMEM((T, D), bf16),
        pltpu.VMEM((T, D), bf16),
        pltpu.VMEM((T, D), bf16),
        pltpu.VMEM((3, T, D), bf16),
        pltpu.VMEM((D, D), bf16),
        pltpu.VMEM((D, D), bf16),
        pltpu.VMEM((NJ, C, BW), bf16),
        pltpu.VMEM((NJ, C, BW), bf16),
        pltpu.VMEM((6, R, D), bf16),
        pltpu.VMEM((R, D), bf16),
        pltpu.VMEM((R, D), f32),
        pltpu.VMEM((R, D), bf16),
        pltpu.VMEM((R, D), bf16),
        pltpu.VMEM((HD + 8, D), f32),
        pltpu.VMEM((BW, C), f32),
        pltpu.VMEM((2, 8, 14, 8, 128), f32),
        pltpu.VMEM((2, 8, 14, 8, 128), f32),
        pltpu.VMEM((2, 8, 14, 8, 128), f32),
        pltpu.VMEM((8, 8, D), f32),
        pltpu.VMEM((8, D), f32),
        pltpu.VMEM((2 * D, C), f32),
        pltpu.VMEM((SLOTS, 4, PIECE, C), f32),
        pltpu.VMEM((LAG, 2, PIECE, 128), f32),
        pltpu.VMEM((LAG, 2, PIECE, 128), f32),
        pltpu.VMEM((LAG, PIECE, 128), f32),
        pltpu.VMEM((LAG, PIECE, 128), f32),
        pltpu.VMEM((2, PIECE, C), f32),
        dma((2,)), dma((2,)), dma((2,)), dma((3,)), dma((3,)), dma((2,)),
        dma((2, 2, 8)), dma((2, 2, 8)), dma((8,)), dma((8,)),
        dma((2, 4)), dma((2, 4)), dma((LAG, 6)), dma((LAG, 6)),
    ]
    y, dx, dw, dgb = pl.pallas_call(
        block,
        name="block",
        out_shape=(jax.ShapeDtypeStruct((T, D), bf16), jax.ShapeDtypeStruct((T, D), bf16),
                   jax.ShapeDtypeStruct((PIECE, 4 * D), f32), jax.ShapeDtypeStruct((8, D), f32)),
        in_specs=[hbm, hbm, hbm, hbm, vmem, vmem],
        out_specs=(hbm, hbm, hbm, vmem),
        scratch_shapes=scratch,
        compiler_params=pltpu.CompilerParams(collective_id=0, has_side_effects=True, vmem_limit_bytes=67043328),
    )(x_tok, dy_tok, w_t, w_out, ln_gamma.reshape(1, D), ln_beta.reshape(1, D))
    return (y, dx, dw[:, D:].reshape(PIECE, 3, NH, HD), dw[:, :D], dgb[0], dgb[1])


def solution(mesh):
    rows = P(("data", "seq"), None)
    return jax.shard_map(
        local_block, mesh=mesh,
        in_specs=(rows, rows, P(None), P(None), P(None, None, None, None), P(None, None)),
        out_specs=(rows, rows, P(("data", "seq"), None, None, None), rows, P("data"), P("data")),
        check_vma=False)
```

time: 501 us -> 250 us (0.50); the launches traced: 492 us -> 250 us
  Pallas kernels: 0 us -> 229 us
  matrix products: 189 us -> 0 us
  waiting for transfers between devices: 139 us -> 0 us
  blocking collectives: 82.8 us -> 0 us
  other arithmetic: 39.5 us -> 0.01 us
  between operations: 14.9 us -> 0.65 us
  local copies, waits for them, and re-layouts: 27.4 us -> 20.1 us
    pallas_call x0 -> x1, Pallas kernels: none -> 229 us  [local_block(): pl.pallas_call(block, name='block', out_shape=(jax.ShapeDtypeStruct((T, D...]
    dot_general x13 -> x0, matrix products: 189 us -> none  [the longest x1 38.9 us: local_block(): jnp.einsum('nc,nf->cf', normed, d_qkv, preferred_element_type=jnp.float32)]
    reduce_scatter x2 -> x0, waiting for transfers between devices: 139 us -> none  [the longest x1 87 us: local_block(): lax.psum_scatter(dwqkv_part, 'seq', scatter_dimension=0, tiled=True)]
    psum x3 -> x0, blocking collectives: 82.8 us -> none  [the longest x1 30.9 us: local_block(): state, norm_vec = lax.psum((state_part, norm_part), 'seq')]
    reduce_sum x4 -> x0, other arithmetic: 24.1 us -> none  [the longest x1 11.2 us: local_block(): dnorm_part = -jnp.sum(correction[:, :, None] * feat_q, axis=0)]
    convert_element_type x1 -> x0, local copies, waits for them, and re-layouts: 20.9 us -> none  [local_block(): jnp.dot(normed, w_flat, preferred_element_type=jnp.float32)]
    convert_element_type x2 -> x0, other arithmetic: 11.4 us -> none  [the longest x1 11.4 us: local_block(): dx_tok = (dy_tok.astype(jnp.float32) + d_ln).astype(jnp.bfloat16)]
    reshape x0 -> x3, local copies, waits for them, and re-layouts: none -> 6.85 us  [the longest x1 4.26 us: local_block(): dw[:, D:].reshape(PIECE, 3, NH, HD)]
  transfers between devices with their start and end apart: 2 -> 0, of which waited for: 2 -> 0; matrix products, arithmetic and copies ran while one was open for 15% -> 0% of each run, Pallas kernels for 0% -> 0%
where the time goes in v1:
time: 250 us
  Pallas kernels  229 us (92%)
  local copies, waits for them, and re-layouts  20.1 us (8%)
    pallas_call x1, Pallas kernels, local_block(): pl.pallas_call(block, name='block', out_shape=(jax.ShapeDtypeStruct((T, D...  229 us
    unnamed x6, local copies, waits for them, and re-layouts  7.63 us

profile of v1, /device:TPU:0, one launch (start us, length us, event | category | flops | bytes accessed | tf_op | source)
XLA Modules:
  0.0 249.6 jit_solution(12730436329550181309)
XLA Ops:
  0.6 1.3 reshape.25.gam
  1.9 1.3 reshape.26.bet
  3.2 228.9 %block.1 = (bf16[2048,1280]{1,0:T(8,128)(2,1)}, bf16[2048,1280]{1,0:T(8,128)(2,1)}, f32[160,5120]{1,0:T(8,128)}, f32[8,1280]{1,0:T(8,128)}) custom-call(bf16[2048,1280]{1,0:T(8,128)(2,1)} %x.1, bf16[2048,1280]{1,0:T(8,128)(2,1)} %dy.1, bf16[3840,1280]{1,0:T(8,128)(2,1)} %bitcast.3, bf16[1280,1280]{1,0:T(8,128)(2,1)} %w_o.1, f32[1,1280]{1,0:T(1,128)} %reshape.25.gam, ...), custom_call_target="tpu_custom_call" | custom-call | tf_op jit(solution)/shard_map/block/pallas_call | solution.py:564
  232.1 1.9 slice.12
  234.0 4.3 %reshape.27 = f32[160,3,16,80]{3,2,1,0:T(8,128)} reshape(f32[160,3840]{1,0:T(8,128)S(1)} %slice.12) | data formatting | bytes 4915200 | tf_op jit(solution)/shard_map/reshape | solution.py:574
  238.2 0.0 slice-start
  238.2 2.2 slice.13
  240.5 1.5 slice_reduce_fusion
  241.9 0.0 slice-start.1
  241.9 5.3 %copy.14 = bf16[2048,1280]{1,0:T(8,128)(2,1)} copy(bf16[2048,1280]{1,0:T(8,128)(2,1)} %get-tuple-element.22) | data formatting | bytes 10485760
  247.2 0.0 slice-done
  247.2 0.0 slice-done.1
  247.2 2.4 copy.15
  (1 shorter events, 0.0 us)
Async XLA Ops:
  238.2 9.0 %slice-start = ((s8[5242880]{0:T(1024)(128)(4,1)}), s8[4194304]{0:T(1024)(128)(4,1)S(1)}, s32[]{:S(2)}) async-start(s8[5242880]{0:T(1024)(128)(4,1)} %bitcast.4), calls=%async_computation | async-start | bytes 8388608
  241.9 5.3 %slice-start.1 = ((s8[5242880]{0:T(1024)(128)(4,1)}), s8[1048576]{0:T(1024)(128)(4,1)S(1)}, s32[]{:S(2)}) async-start(s8[5242880]{0:T(1024)(128)(4,1)} %bitcast.4), calls=%async_computation.1 | async-start | bytes 2097152

commit v2 on v1

--- a/solution.py
+++ b/solution.py
@@ -13,6 +13,7 @@
 HD = 80
 NH = 16
 R = 256
+G = 32
 NT_ = T // R
 C = 256
 NJ = D // C
@@ -57,9 +58,9 @@
 
 
 def block(x, dy, w_t, w_o, gam, bet,
-          y, dx, dw, dgb,
+          y, dx, dwq, dwo, dgam, dbet,
           u_s, g_s, o_s, qkv_s, wo_s, bd_s, zb_s, on_s, tile_s,
-          f_s, acc_s, ph_s, pl_s, c_s, st_s, part_s, rsr_s, ag_s, gbr_s, gb_s,
+          f_s, acc_s, den_s, ph_s, pl_s, c_s, part_s, rsr_s, ags_s, agd_s, gbr_s, gb_s,
           p_s, r1_s, ra_s, rb_s, ra2_s, rb2_s, ost_s,
           xsem, dsem, ysem, wsem, lsem, osem, ar_send, ar_recv, gb_send, gb_recv,
           dd_send, dd_recv, ln_send, ln_recv):
@@ -102,32 +103,32 @@
     x_in(0).start()
     w_in(0).start()
     w_in(1).start()
-    dy_all.start()
-    wo_all.start()
 
     barrier = pltpu.get_barrier_semaphore()
     for k in range(1, 8):
         pl.semaphore_signal(barrier, inc=1, device_id={"seq": (s + k) % 8}, device_id_type=pl.DeviceIdType.MESH)
-    pl.semaphore_wait(barrier, 7)
 
     def pack(a):
         for m in range(110):
             r0, c0 = 8 * (m // 10), 128 * (m % 10)
-            part_s[a, m // 14, m % 14] = c_s[r0:r0 + 8, c0:c0 + 128]
+            part_s[m // 14, m % 14] = c_s[r0:r0 + 8, c0:c0 + 128]
         for m in range(110, 112):
-            part_s[a, m // 14, m % 14] = jnp.zeros((8, 128), f32)
+            part_s[m // 14, m % 14] = jnp.zeros((8, 128), f32)
+
+    def ag(a):
+        return agd_s if a else ags_s
 
     def ar_copy(a, phase, k):
         tgt = (s + k) % 8
         if phase == 0:
-            return remote(part_s.at[a, tgt], rsr_s.at[a, s], ar_send.at[a, 0, k], ar_recv.at[a, 0, k], tgt)
-        return remote(ag_s.at[a, s], ag_s.at[a, s], ar_send.at[a, 1, k], ar_recv.at[a, 1, k], tgt)
+            return remote(part_s.at[tgt], rsr_s.at[s], ar_send.at[a, 0, k], ar_recv.at[a, 0, k], tgt)
+        return remote(ag(a).at[s], ag(a).at[s], ar_send.at[a, 1, k], ar_recv.at[a, 1, k], tgt)
 
     def ar_land(a, phase, k):
         src = (s + 8 - k) % 8
         if phase == 0:
-            return remote(part_s.at[a, src], rsr_s.at[a, src], ar_send.at[a, 0, k], ar_recv.at[a, 0, k], src)
-        return remote(ag_s.at[a, src], ag_s.at[a, src], ar_send.at[a, 1, k], ar_recv.at[a, 1, k], src)
+            return remote(part_s.at[src], rsr_s.at[src], ar_send.at[a, 0, k], ar_recv.at[a, 0, k], src)
+        return remote(ag(a).at[src], ag(a).at[src], ar_send.at[a, 1, k], ar_recv.at[a, 1, k], src)
 
     def ar_start(a):
         pack(a)
@@ -135,11 +136,11 @@
             ar_copy(a, 0, k).start()
 
     def ar_mid(a):
-        total = part_s[a, s]
+        total = part_s[s]
         for k in range(1, 8):
             ar_land(a, 0, k).wait_recv()
-            total = total + rsr_s[a, (s + 8 - k) % 8]
-        ag_s[a, s] = total
+            total = total + rsr_s[(s + 8 - k) % 8]
+        ag(a)[s] = total.astype(ag(a).dtype)
         for k in range(1, 8):
             ar_copy(a, 1, k).start()
 
@@ -151,7 +152,7 @@
             ar_copy(a, 1, k).wait_send()
         for m in range(110):
             r0, c0 = 8 * (m // 10), 128 * (m % 10)
-            c_s[r0:r0 + 8, c0:c0 + 128] = ag_s[a, m // 14, m % 14]
+            c_s[r0:r0 + 8, c0:c0 + 128] = ag(a)[m // 14, m % 14].astype(f32)
 
     def compact(ref, base, j):
         head = head_of(lax.broadcasted_iota(jnp.int32, (HD, C), 1) + C * j)
@@ -211,15 +212,16 @@
         link(i, 4).start()
         link(i, 5).start()
 
-    def piece_out(i):
-        return pltpu.make_async_copy(ost_s.at[i % 2], dw.at[:, cols(i)], osem.at[i % 2])
+    def piece_out(i, first=False):
+        dst = dwo.at[:, cols(i)] if first else dwq.at[:, cols(i - NJ)]
+        return pltpu.make_async_copy(ost_s.at[i % 2], dst, osem.at[i % 2])
 
     def last_sum(i):
         slot, q = i % SLOTS, i % LAG
 
         @pl.when(i >= 2)
         def _():
-            piece_out(i - 2).wait()
+            pltpu.make_async_copy(ost_s.at[i % 2], dwq.at[:, 0:C], osem.at[i % 2]).wait()
 
         link(i, 4).wait_recv()
         ost_s[i % 2, :, 0:128] = r1_s[slot, 2 * py + px, :, 0:128] + ra2_s[q]
@@ -227,7 +229,14 @@
         ost_s[i % 2, :, 128:256] = r1_s[slot, 2 * py + px, :, 128:256] + rb2_s[q]
         for n in range(6):
             link(i, n).wait_send()
-        piece_out(i).start()
+
+        @pl.when(i < NJ)
+        def _():
+            piece_out(i, True).start()
+
+        @pl.when(i >= NJ)
+        def _():
+            piece_out(i).start()
 
     def pump(m, lo, hi):
         @pl.when((m - 4 >= lo) & (m - 4 < hi))
@@ -242,9 +251,8 @@
         def _():
             first_hop(m)
 
-    bd_s[...] = jnp.zeros((D, D), bf16)
-    gamma = gam[...]
-    beta = bet[...]
+    gamma = gam[...].reshape(1, D)
+    beta = bet[...].reshape(1, D)
 
     @pl.loop(0, NT_)
     def _(t):
@@ -254,56 +262,59 @@
         def _():
             x_in(t + 1).start()
 
-        x_hat, _ = normalise(tile_s[t % 2].astype(f32))
-        u_s[rows(t), :] = (x_hat * gamma + beta).astype(bf16)
-
+        for g in range(R // G):
+            x_hat, _ = normalise(tile_s[t % 2, G * g:G * g + G, :].astype(f32))
+            u_s[pl.ds(pl.multiple_of(t * R + G * g, G), G), :] = (x_hat * gamma + beta).astype(bf16)
+
+    dy_all.start()
+    wo_all.start()
+
+    def project(n, which, keep):
+        w_in(n).wait()
+
+        @pl.when(n + 2 < 3 * NJ)
+        def _():
+            w_in(n + 2).start()
+
+        j = n % NJ
+        out = dot_nt(u_s[...], tile_s[2 + n % 3]).astype(bf16)
+        qkv_s[which, :, cols(j)] = out
+        if keep:
+            feat = phi(out.astype(f32)).astype(bf16)
+            o_s[:, cols(j)] = feat
+            c_s[HD:HD + 1, cols(j)] = jnp.sum(feat.astype(f32), axis=0, keepdims=True)
+
+    c_s[HD:HD + 8, :] = jnp.zeros((8, D), f32)
+
+    @pl.loop(0, NJ)
+    def _(n):
+        project(n, 1, True)
+
+    @pl.loop(NJ, 2 * NJ)
+    def _(n):
+        project(n, 2, False)
+
+    for j in range(NJ):
+        p_s[BW * j:BW * j + BW, :] = dot_tn(o_s[:, BAND[j]:BAND[j] + BW], qkv_s[2, :, C * j:C * j + C])
+        compact(p_s, BW * j, j)
+    pl.semaphore_wait(barrier, 7)
+    ar_start(0)
+
+    @pl.loop(2 * NJ, 3 * NJ - 2)
+    def _(n):
+        project(n, 0, False)
+
+    ar_mid(0)
+    @pl.loop(3 * NJ - 2, 3 * NJ)
+    def _(n):
+        project(n, 0, False)
+
+    bd_s[...] = jnp.zeros((D, D), bf16)
     for j in range(NJ):
         hr = head_of(lax.broadcasted_iota(jnp.int32, (C, BW), 0) + C * j)
         hc = head_of(lax.broadcasted_iota(jnp.int32, (C, BW), 1) + BAND[j])
         on_s[j] = jnp.where(hr == hc, 1.0, 0.0).astype(bf16)
 
-    def project(n, which, keep):
-        w_in(n).wait()
-
-        @pl.when(n + 2 < 3 * NJ)
-        def _():
-            w_in(n + 2).start()
-
-        j = n % NJ
-
-        @pl.loop(0, T // 512)
-        def _(b):
-            r = pl.ds(pl.multiple_of(b * 512, 512), 512)
-            out = dot_nt(u_s[r, :], tile_s[2 + n % 3]).astype(bf16)
-            qkv_s[which, r, cols(j)] = out
-            if keep:
-                feat = phi(out.astype(f32)).astype(bf16)
-                o_s[r, cols(j)] = feat
-                part = jnp.sum(feat.astype(f32), axis=0, keepdims=True)
-                before = jnp.where(b == 0, 0.0, c_s[HD:HD + 1, cols(j)])
-                c_s[HD:HD + 1, cols(j)] = before + part
-
-    c_s[HD:HD + 8, :] = jnp.zeros((8, D), f32)
-
-    @pl.loop(0, NJ)
-    def _(n):
-        project(n, 1, True)
-
-    @pl.loop(NJ, 2 * NJ)
-    def _(n):
-        project(n, 2, False)
-
-    for j in range(NJ):
-        st_s[...] = dot_tn(o_s[:, BAND[j]:BAND[j] + BW], qkv_s[2, :, C * j:C * j + C])
-        compact(st_s, 0, j)
-    ar_start(0)
-
-    @pl.loop(2 * NJ, 3 * NJ - 1)
-    def _(n):
-        project(n, 0, False)
-
-    ar_mid(0)
-    project(3 * NJ - 1, 0, False)
     ar_end(0)
     expand()
     for j in range(NJ):
@@ -334,16 +345,16 @@
 
         to_mate(i)
 
-        @pl.when(i == 1)
-        def _():
-            pump(0, 0, NJ)
+        @pl.when((i == 1) | (i == 3))
+        def _():
+            first_hop((i - 1) // 2)
 
     chip_sum(NJ - 1)
-    pump(1, 0, NJ)
+    second_hop(0)
+    first_hop(2)
 
     p_s[...] = jnp.zeros((2 * D, C), f32)
-    st_s[0:8, 0:C] = jnp.zeros((8, C), f32)
-    gb_s[...] = jnp.zeros((8, D), f32)
+    gb_s[...] = jnp.zeros((2, 8, D), f32)
 
     @pl.loop(0, NT_)
     def _(t):
@@ -351,10 +362,15 @@
         f_s[...] = phi(qkv_s[0, rows(t), :].astype(f32)).astype(bf16)
         for j in range(NJ):
             cj = slice(C * j, C * j + C)
-            num, den = num_den(j)
-            g = (acc_s[:, cj] / den).astype(bf16)
-            g_s[rows(t), cj] = g
-            prod = g.astype(f32) * (num / den)
+            den = dot_nt(f_s[:, BAND[j]:BAND[j] + BW], zb_s[j])
+            den_s[:, cj] = den
+            g_s[rows(t), cj] = (acc_s[:, cj] / den).astype(bf16)
+        for j in range(NJ):
+            cj = slice(C * j, C * j + C)
+            band = slice(BAND[j], BAND[j] + BW)
+            back = dot_nt(g_s[rows(t), band], bd_s[cj, band])
+            acc_s[:, cj] = back
+            prod = f_s[:, cj].astype(f32) / den_s[:, cj] * back
             high = prod.astype(bf16)
             ph_s[:, cj] = high
             pl_s[:, cj] = (prod - high.astype(f32)).astype(bf16)
@@ -362,25 +378,21 @@
             cj = slice(C * j, C * j + C)
             band = slice(BAND[j], BAND[j] + BW)
             corr = dot_nt(ph_s[:, band], on_s[j]) + dot_nt(pl_s[:, band], on_s[j])
-            d_f = dot_nt(g_s[rows(t), band], bd_s[cj, band]) - corr * c_s[HD:HD + 1, cj].astype(bf16).astype(f32)
+            d_f = acc_s[:, cj] - corr * c_s[HD:HD + 1, cj].astype(bf16).astype(f32)
             raw = qkv_s[0, rows(t), cj].astype(f32)
             qkv_s[0, rows(t), cj] = (d_f * slope(raw)).astype(bf16)
-            gb_s[0:1, cj] = gb_s[0:1, cj] + jnp.sum(corr * f_s[:, cj].astype(f32), axis=0, keepdims=True)
+            gb_s[0, 0:1, cj] = gb_s[0, 0:1, cj] + jnp.sum(corr * f_s[:, cj].astype(f32), axis=0, keepdims=True)
             p_s[BW * j:BW * j + BW, :] = p_s[BW * j:BW * j + BW, :] + dot_tn(f_s[:, band], g_s[rows(t), cj])
 
         @pl.when(t % 2 == 1)
         def _():
-            pump(2 + t // 2, 0, NJ)
+            pump(3 + t // 2, 0, NJ)
 
     for j in range(NJ):
         compact(p_s, BW * j, j)
-    c_s[HD:HD + 1, :] = -gb_s[0:1, :]
+    c_s[HD:HD + 1, :] = -gb_s[0, 0:1, :]
     ar_start(1)
     wt_hi.start()
-
-    @pl.loop(6, 9)
-    def _(m):
-        pump(m, 0, NJ)
 
     def weight_chunk(i):
         n = i - NJ
@@ -398,35 +410,18 @@
 
         @pl.when((i == NJ + 1) | (i == NJ + 3))
         def _():
-            pump(NJ + (i - NJ) // 2, NJ, NCH)
+            first_hop(NJ + (i - NJ) // 2)
+
+        @pl.when(i < NJ + 2)
+        def _():
+            last_sum(i - 2)
+
+        @pl.when(i == NJ + 2)
+        def _():
+            ar_mid(1)
 
     chip_sum(2 * NJ - 1)
-    ar_mid(1)
-
-    x_in(0).start()
-
-    @pl.loop(0, NT_)
-    def _(t):
-        x_in(t).wait()
-
-        @pl.when(t + 1 < NT_)
-        def _():
-            x_in(t + 1).start()
-
-        @pl.when(t >= 2)
-        def _():
-            tile_out(y, t - 2).wait()
-
-        tile_s[4 + t % 2] = (tile_s[t % 2].astype(f32) + dot_nn(o_s[rows(t), :], wo_s[...])).astype(bf16)
-        tile_out(y, t).start()
-
-        @pl.when(t % 4 == 3)
-        def _():
-            pump(NJ + 2 + t // 4, NJ, NCH)
-
-    wt_lo.start()
-    tile_out(y, NT_ - 2).wait()
-    tile_out(y, NT_ - 1).wait()
+
     ar_end(1)
     expand()
 
@@ -442,32 +437,66 @@
             qkv_s[1, rows(t), cj] = (d_f * slope(raw)).astype(bf16)
             qkv_s[2, rows(t), cj] = dot_nn(f_s[:, band], bd_s[band, cj]).astype(bf16)
 
-        @pl.when(t == 3)
-        def _():
-            pump(NJ + 4, NJ, NCH)
-
-    @pl.loop(2 * NJ, 2 * NJ + 2)
-    def _(i):
-        weight_chunk(i)
-
-        @pl.when(i > 2 * NJ)
-        def _():
+        @pl.when(t % 3 == 1)
+        def _():
+            pump(NJ + 2 + t // 3, NJ, NCH)
+
+    x_in(0).start()
+    weight_chunk(2 * NJ)
+    to_mate(2 * NJ)
+
+    @pl.loop(0, NT_)
+    def _(t):
+        @pl.when(t % 2 == 0)
+        def _():
+            i = 2 * NJ + 1 + t // 2
+            weight_chunk(i)
             chip_sum(i - 1)
-
-        to_mate(i)
-
-    gb_s[...] = jnp.zeros((8, D), f32)
+            to_mate(i)
+            pump(i - 1, NJ, NCH)
+
+        x_in(t).wait()
+
+        @pl.when(t + 1 < NT_)
+        def _():
+            x_in(t + 1).start()
+
+        @pl.when(t >= 2)
+        def _():
+            tile_out(y, t - 2).wait()
+
+        tile_s[4 + t % 2] = (tile_s[t % 2].astype(f32) + dot_nn(o_s[rows(t), :], wo_s[...])).astype(bf16)
+        tile_out(y, t).start()
+
+    wt_lo.start()
+    tile_out(y, NT_ - 2).wait()
+    tile_out(y, NT_ - 1).wait()
+
+    gb_s[...] = jnp.zeros((2, 8, D), f32)
     x_in(0).start()
     dy_in(0).start()
-    wt_lo.wait()
-    wt_hi.wait()
 
     @pl.loop(0, NT_)
     def _(t):
-        pump(2 * NJ + t, NJ, NCH)
-        weight_chunk(2 * NJ + 2 + t)
-        chip_sum(2 * NJ + 1 + t)
-        to_mate(2 * NJ + 2 + t)
+        @pl.when(t < NJ)
+        def _():
+            weight_chunk(3 * NJ + t)
+
+        @pl.when(t <= NJ)
+        def _():
+            chip_sum(3 * NJ - 1 + t)
+
+        @pl.when(t < NJ)
+        def _():
+            to_mate(3 * NJ + t)
+
+        pump(3 * NJ - 1 + t, NJ, NCH)
+
+        @pl.when(t == 0)
+        def _():
+            wt_lo.wait()
+            wt_hi.wait()
+
         x_in(t).wait()
         dy_in(t).wait()
 
@@ -481,32 +510,38 @@
             tile_out(dx, t - 2).wait()
 
         cut = T - D
-        for j in range(NJ):
-            cj = slice(C * j, C * j + C)
+
+        @pl.loop(0, NJ)
+        def _(j):
+            cj = cols(j)
             acc_s[:, cj] = (dot_nn(qkv_s[0, rows(t), :], o_s[0:D, cj])
                             + dot_nn(qkv_s[1, rows(t), 0:cut], o_s[D:T, cj])
                             + dot_nn(qkv_s[1, rows(t), cut:D], g_s[0:D - cut, cj])
                             + dot_nn(qkv_s[2, rows(t), :], g_s[D - cut:2 * D - cut, cj]))
-        du = acc_s[...]
-        x_hat, inv = normalise(tile_s[t % 2].astype(f32))
-        dux = du * x_hat
-        gb_s[0:1, :] = gb_s[0:1, :] + jnp.sum(dux, axis=0, keepdims=True)
-        gb_s[1:2, :] = gb_s[1:2, :] + jnp.sum(du, axis=0, keepdims=True)
-        e = du * gamma
-        m1 = jnp.mean(e, axis=-1, keepdims=True)
-        m2 = jnp.mean(e * x_hat, axis=-1, keepdims=True)
-        tile_s[4 + t % 2] = (tile_s[2 + t % 2].astype(f32) + inv * (e - m1 - x_hat * m2)).astype(bf16)
+
+        for g in range(R // G):
+            gs = slice(G * g, G * g + G)
+            x_hat, inv = normalise(tile_s[t % 2, gs, :].astype(f32))
+            du = acc_s[gs, :]
+            dux = du * x_hat
+            gb_s[0] = gb_s[0] + sum(dux[8 * q:8 * q + 8, :] for q in range(G // 8))
+            gb_s[1] = gb_s[1] + sum(du[8 * q:8 * q + 8, :] for q in range(G // 8))
+            e = du * gamma
+            m1 = jnp.mean(e, axis=-1, keepdims=True)
+            m2 = jnp.mean(e * x_hat, axis=-1, keepdims=True)
+            tile_s[4 + t % 2, gs, :] = (tile_s[2 + t % 2, gs, :].astype(f32) + inv * (e - m1 - x_hat * m2)).astype(bf16)
+
         tile_out(dx, t).start()
 
     def gb_copy(k):
-        return remote(gb_s, gbr_s.at[k], gb_send.at[k], gb_recv.at[k], (s + k) % 8)
-
+        return remote(gbr_s.at[0], gbr_s.at[k], gb_send.at[k], gb_recv.at[k], (s + k) % 8)
+
+    for n in range(2):
+        gbr_s[0, n:n + 1, :] = jnp.sum(gb_s[n], axis=0, keepdims=True)
     for k in range(1, 8):
         gb_copy(k).start()
-    pump(NCH - 2, NJ, NCH)
-    chip_sum(NCH - 1)
-
-    @pl.loop(NCH - 1, NCH + 4)
+
+    @pl.loop(NCH + 2, NCH + 4)
     def _(m):
         pump(m, NJ, NCH)
 
@@ -515,11 +550,11 @@
     for k in range(1, 8):
         gb_copy(k).wait_recv()
         gb_copy(k).wait_send()
-    gbr_s[0] = gb_s[...]
-    total = jnp.zeros((8, D), f32)
+    total = jnp.zeros((2, D), f32)
     for d in range(8):
         total = total + gbr_s[(s + 8 - d) % 8]
-    dgb[...] = total
+    dgam[...] = total[0]
+    dbet[...] = total[1]
     piece_out(NCH - 2).wait()
     piece_out(NCH - 1).wait()
 
@@ -541,15 +576,16 @@
         pltpu.VMEM((6, R, D), bf16),
         pltpu.VMEM((R, D), bf16),
         pltpu.VMEM((R, D), f32),
+        pltpu.VMEM((R, D), f32),
         pltpu.VMEM((R, D), bf16),
         pltpu.VMEM((R, D), bf16),
         pltpu.VMEM((HD + 8, D), f32),
-        pltpu.VMEM((BW, C), f32),
-        pltpu.VMEM((2, 8, 14, 8, 128), f32),
-        pltpu.VMEM((2, 8, 14, 8, 128), f32),
-        pltpu.VMEM((2, 8, 14, 8, 128), f32),
-        pltpu.VMEM((8, 8, D), f32),
-        pltpu.VMEM((8, D), f32),
+        pltpu.VMEM((8, 14, 8, 128), f32),
+        pltpu.VMEM((8, 14, 8, 128), f32),
+        pltpu.VMEM((8, 14, 8, 128), bf16),
+        pltpu.VMEM((8, 14, 8, 128), f32),
+        pltpu.VMEM((8, 2, D), f32),
+        pltpu.VMEM((2, 8, D), f32),
         pltpu.VMEM((2 * D, C), f32),
         pltpu.VMEM((SLOTS, 4, PIECE, C), f32),
         pltpu.VMEM((LAG, 2, PIECE, 128), f32),
@@ -561,17 +597,18 @@
         dma((2, 2, 8)), dma((2, 2, 8)), dma((8,)), dma((8,)),
         dma((2, 4)), dma((2, 4)), dma((LAG, 6)), dma((LAG, 6)),
     ]
-    y, dx, dw, dgb = pl.pallas_call(
+    y, dx, dwq, dwo, dgam, dbet = pl.pallas_call(
         block,
         name="block",
         out_shape=(jax.ShapeDtypeStruct((T, D), bf16), jax.ShapeDtypeStruct((T, D), bf16),
-                   jax.ShapeDtypeStruct((PIECE, 4 * D), f32), jax.ShapeDtypeStruct((8, D), f32)),
+                   jax.ShapeDtypeStruct((PIECE, 3 * D), f32), jax.ShapeDtypeStruct((PIECE, D), f32),
+                   jax.ShapeDtypeStruct((D,), f32), jax.ShapeDtypeStruct((D,), f32)),
         in_specs=[hbm, hbm, hbm, hbm, vmem, vmem],
-        out_specs=(hbm, hbm, hbm, vmem),
+        out_specs=(hbm, hbm, hbm, hbm, vmem, vmem),
         scratch_shapes=scratch,
         compiler_params=pltpu.CompilerParams(collective_id=0, has_side_effects=True, vmem_limit_bytes=67043328),
-    )(x_tok, dy_tok, w_t, w_out, ln_gamma.reshape(1, D), ln_beta.reshape(1, D))
-    return (y, dx, dw[:, D:].reshape(PIECE, 3, NH, HD), dw[:, :D], dgb[0], dgb[1])
+    )(x_tok, dy_tok, w_t, w_out, ln_gamma, ln_beta)
+    return (y, dx, dwq.reshape(PIECE, 3, NH, HD), dwo, dgam, dbet)
 
 
 def solution(mesh):

time: 250 us -> 204 us (0.82)
  Pallas kernels: 229 us -> 187 us
  local copies, waits for them, and re-layouts: 20.1 us -> 15.6 us
    pallas_call x1, Pallas kernels: 229 us -> 187 us  [local_block(): pl.pallas_call(block, name='block', out_shape=(jax.ShapeDtypeStruct((T, D...]
    slice x3 -> x0, local copies, waits for them, and re-layouts: 5.57 us -> none  [the longest x1 2.24 us: local_block(): dw[:, :D]]
    unnamed x6 -> x15, local copies, waits for them, and re-layouts: 7.63 us -> 9.8 us
    reshape x3 -> x1, local copies, waits for them, and re-layouts: 6.85 us -> 5.83 us  [local_block(): return (y, dx, dwq.reshape(PIECE, 3, NH, HD), dwo, dgam, dbet)]
where the time goes in v2:
time: 204 us; the launch traced here: 203 us
  Pallas kernels  187 us (92%)
  local copies, waits for them, and re-layouts  15.6 us (8%)
    pallas_call x1, Pallas kernels, local_block(): pl.pallas_call(block, name='block', out_shape=(jax.ShapeDtypeStruct((T, D...  187 us
    unnamed x15, local copies, waits for them, and re-layouts  9.8 us
    reshape x1, local copies, waits for them, and re-layouts, local_block(): return (y, dx, dwq.reshape(PIECE, 3, NH, HD), dwo, dgam, dbet)  5.83 us

profile of v2, /device:TPU:0, one launch (start us, length us, event | category | flops | bytes accessed | tf_op | source)
XLA Modules:
  0.0 202.9 jit_solution(6981363962680992180)
XLA Ops:
  0.6 186.6 %block.1 = (bf16[2048,1280]{1,0:T(8,128)(2,1)}, bf16[2048,1280]{1,0:T(8,128)(2,1)}, f32[160,3840]{1,0:T(8,128)}, f32[160,1280]{1,0:T(8,128)}, f32[1280]{0:T(1024)}, /*index=5*/f32[1280]{0:T(1024)}) custom-call(bf16[2048,1280]{1,0:T(8,128)(2,1)} %x.1, bf16[2048,1280]{1,0:T(8,128)(2,1)} %dy.1, bf16[3840,1280]{1,0:T(8,128)(2,1)} %bitcast.3, ...), custom_call_target="tpu_custom_call" | custom-call | tf_op jit(solution)/shard_map/block/pallas_call | solution.py:600
  187.3 0.0 slice-start
  187.3 5.8 %reshape.19 = f32[160,3,16,80]{3,2,1,0:T(8,128)} reshape(f32[160,3840]{1,0:T(8,128)} %get-tuple-element.14) | data formatting | bytes 4915200 | tf_op jit(solution)/shard_map/reshape | solution.py:611
  193.1 0.0 slice-start.1
  193.1 5.3 %copy.17 = bf16[2048,1280]{1,0:T(8,128)(2,1)} copy(bf16[2048,1280]{1,0:T(8,128)(2,1)} %get-tuple-element.24) | data formatting | bytes 10485760
  198.5 0.0 slice-done
  198.5 0.0 slice-done.1
  198.5 0.0 copy-start
  198.5 0.0 copy-start.2
  198.5 0.0 copy-start.1
  198.5 2.4 %copy.18 = bf16[2048,1280]{1,0:T(8,128)(2,1)} copy(bf16[2048,1280]{1,0:T(8,128)(2,1)S(1)} %bitcast.5) | data formatting | bytes 10485760
  200.8 0.0 copy-done
  200.8 0.9 copy.19
  201.7 0.0 copy-done.2
  201.7 0.6 copy.20
  202.3 0.0 copy-done.1
  202.3 0.6 copy.21
  (1 shorter events, 0.0 us)
Async XLA Ops:
  187.3 11.2 %slice-start = ((s8[5242880]{0:T(1024)(128)(4,1)}), s8[1048576]{0:T(1024)(128)(4,1)S(1)}, s32[]{:S(2)}) async-start(s8[5242880]{0:T(1024)(128)(4,1)} %bitcast.4), calls=%async_computation | async-start | bytes 2097152
  193.1 5.3 %slice-start.1 = ((s8[5242880]{0:T(1024)(128)(4,1)}), s8[4194304]{0:T(1024)(128)(4,1)S(1)}, s32[]{:S(2)}) async-start(s8[5242880]{0:T(1024)(128)(4,1)} %bitcast.4), calls=%async_computation.1 | async-start | bytes 8388608
  198.5 2.4 %copy-start = (f32[160,1280]{1,0:T(8,128)S(1)}, f32[160,1280]{1,0:T(8,128)}, u32[]{:S(2)}) copy-start(f32[160,1280]{1,0:T(8,128)} %get-tuple-element.27) | copy-start | bytes 2457604
  198.5 3.3 %copy-start.2 = (f32[1280]{0:T(1024)S(1)}, f32[1280]{0:T(1024)}, u32[]{:S(2)}) copy-start(f32[1280]{0:T(1024)} %get-tuple-element.28) | copy-start | bytes 15364
  198.5 3.9 %copy-start.1 = (f32[1280]{0:T(1024)S(1)}, f32[1280]{0:T(1024)}, u32[]{:S(2)}) copy-start(f32[1280]{0:T(1024)} %get-tuple-element.29) | copy-start | bytes 15364

commit v3 on v2

--- a/solution.py
+++ b/solution.py
@@ -60,9 +60,9 @@
 def block(x, dy, w_t, w_o, gam, bet,
           y, dx, dwq, dwo, dgam, dbet,
           u_s, g_s, o_s, qkv_s, wo_s, bd_s, zb_s, on_s, tile_s,
-          f_s, acc_s, den_s, ph_s, pl_s, c_s, part_s, rsr_s, ags_s, agd_s, gbr_s, gb_s,
+          f_s, acc_s, den_s, ph_s, pl_s, c_s, zz_s, part_s, rsr_s, ag_s, gbr_s, gb_s,
           p_s, r1_s, ra_s, rb_s, ra2_s, rb2_s, ost_s,
-          xsem, dsem, ysem, wsem, lsem, osem, ar_send, ar_recv, gb_send, gb_recv,
+          fsem, xsem, dsem, ysem, wsem, lsem, osem, z_send, z_recv, ar_send, ar_recv, gb_send, gb_recv,
           dd_send, dd_recv, ln_send, ln_recv):
     s = lax.axis_index("seq")
     core = s % 2
@@ -82,77 +82,105 @@
     def cols(j):
         return pl.ds(pl.multiple_of(j * C, C), C)
 
+    def slot(n):
+        return pl.ds(pl.multiple_of(n * R, R), R)
+
     def x_in(t):
-        return pltpu.make_async_copy(x.at[rows(t), :], tile_s.at[t % 2], xsem.at[t % 2])
+        return pltpu.make_async_copy(x.at[rows(t), :], tile_s.at[slot(t % 2), :], xsem.at[t % 2])
 
     def dy_in(t):
-        return pltpu.make_async_copy(dy.at[rows(t), :], tile_s.at[2 + t % 2], dsem.at[t % 2])
+        return pltpu.make_async_copy(dy.at[rows(t), :], tile_s.at[slot(2 + t % 2), :], dsem.at[t % 2])
 
     def tile_out(dst, t):
-        return pltpu.make_async_copy(tile_s.at[4 + t % 2], dst.at[rows(t), :], ysem.at[t % 2])
+        return pltpu.make_async_copy(tile_s.at[slot(4 + t % 2), :], dst.at[rows(t), :], ysem.at[t % 2])
 
     def w_in(n):
-        r = pl.multiple_of(((n + NJ) % (3 * NJ)) * C, C)
-        return pltpu.make_async_copy(w_t.at[pl.ds(r, C), :], tile_s.at[2 + n % 3], wsem.at[n % 3])
+        def ge(k):
+            return int(n >= k) if isinstance(n, int) else (n >= k).astype(jnp.int32)
+
+        r = n + 5 + 2 * ge(3) - 4 * ge(5) + 2 * ge(7) - 15 * ge(10)
+        return pltpu.make_async_copy(w_t.at[cols(r), :], tile_s.at[slot(2 + n % 3), :], wsem.at[n % 3])
 
     dy_all = pltpu.make_async_copy(dy, g_s, lsem.at[0])
     wo_all = pltpu.make_async_copy(w_o, wo_s, lsem.at[1])
     wt_lo = pltpu.make_async_copy(w_t.at[pl.ds(0, T), :], o_s, lsem.at[2])
     wt_hi = pltpu.make_async_copy(w_t.at[pl.ds(T, 3 * D - T), :], g_s.at[pl.ds(0, 3 * D - T), :], lsem.at[0])
 
-    x_in(0).start()
-    w_in(0).start()
-    w_in(1).start()
+    def x_first(t):
+        return pltpu.make_async_copy(x.at[rows(t), :], qkv_s.at[0, rows(t), :], fsem.at[t])
+
+    for t in range(NT_):
+        x_first(t).start()
+        if t == 1:
+            w_in(0).start()
+            w_in(1).start()
 
     barrier = pltpu.get_barrier_semaphore()
     for k in range(1, 8):
         pl.semaphore_signal(barrier, inc=1, device_id={"seq": (s + k) % 8}, device_id_type=pl.DeviceIdType.MESH)
 
-    def pack(a):
-        for m in range(110):
-            r0, c0 = 8 * (m // 10), 128 * (m % 10)
-            part_s[m // 14, m % 14] = c_s[r0:r0 + 8, c0:c0 + 128]
-        for m in range(110, 112):
-            part_s[m // 14, m % 14] = jnp.zeros((8, 128), f32)
-
-    def ag(a):
-        return agd_s if a else ags_s
-
-    def ar_copy(a, phase, k):
-        tgt = (s + k) % 8
+    tiles = [[(r, c) for r in range(10) for c in cs] for cs in (range(4), range(4, 10), range(10))]
+    share = ((0, 5), (5, 13), (0, 13))
+
+    def place(a, m):
+        lo, hi = share[a]
+        return m // (hi - lo), lo + m % (hi - lo)
+
+    def ar_copy(a, phase, k, landing=False):
+        dev = (s + 8 - k) % 8 if landing else (s + k) % 8
+        lo, hi = share[a]
+        sems = ar_send.at[a, phase, k], ar_recv.at[a, phase, k], dev
         if phase == 0:
-            return remote(part_s.at[tgt], rsr_s.at[s], ar_send.at[a, 0, k], ar_recv.at[a, 0, k], tgt)
-        return remote(ag(a).at[s], ag(a).at[s], ar_send.at[a, 1, k], ar_recv.at[a, 1, k], tgt)
-
-    def ar_land(a, phase, k):
-        src = (s + 8 - k) % 8
-        if phase == 0:
-            return remote(part_s.at[src], rsr_s.at[src], ar_send.at[a, 0, k], ar_recv.at[a, 0, k], src)
-        return remote(ag(a).at[src], ag(a).at[src], ar_send.at[a, 1, k], ar_recv.at[a, 1, k], src)
+            row = dev if landing else s
+            return remote(part_s.at[dev, lo:hi], rsr_s.at[row, lo:hi], *sems)
+        row = dev if landing else s
+        return remote(ag_s.at[row, lo:hi], ag_s.at[row, lo:hi], *sems)
+
+    def z_copy(b, k, landing=False):
+        dev = (s + 8 - k) % 8 if landing else (s + k) % 8
+        row = dev if landing else s
+        return remote(zz_s.at[b, row], zz_s.at[b, row], z_send.at[b, k], z_recv.at[b, k], dev)
+
+    def z_start(b):
+        for k in range(1, 8):
+            z_copy(b, k).start()
+
+    def z_end(b):
+        for k in range(1, 8):
+            z_copy(b, k, True).wait_recv()
+        for k in range(1, 8):
+            z_copy(b, k).wait_send()
+        total = zz_s[b, 0]
+        for d in range(1, 8):
+            total = total + zz_s[b, d]
+        c_s[HD:HD + 1, :] = total
 
     def ar_start(a):
-        pack(a)
+        for m, (r, c) in enumerate(tiles[a]):
+            d, p = place(a, m)
+            part_s[d, p] = c_s[8 * r:8 * r + 8, 128 * c:128 * c + 128]
         for k in range(1, 8):
             ar_copy(a, 0, k).start()
 
     def ar_mid(a):
-        total = part_s[s]
-        for k in range(1, 8):
-            ar_land(a, 0, k).wait_recv()
-            total = total + rsr_s[(s + 8 - k) % 8]
-        ag(a)[s] = total.astype(ag(a).dtype)
+        lo, hi = share[a]
+        total = part_s[s, lo:hi]
+        for k in range(1, 8):
+            ar_copy(a, 0, k, True).wait_recv()
+            total = total + rsr_s[(s + 8 - k) % 8, lo:hi]
+        ag_s[s, lo:hi] = total.astype(bf16)
         for k in range(1, 8):
             ar_copy(a, 1, k).start()
 
     def ar_end(a):
         for k in range(1, 8):
-            ar_land(a, 1, k).wait_recv()
+            ar_copy(a, 1, k, True).wait_recv()
         for k in range(1, 8):
             ar_copy(a, 0, k).wait_send()
             ar_copy(a, 1, k).wait_send()
-        for m in range(110):
-            r0, c0 = 8 * (m // 10), 128 * (m % 10)
-            c_s[r0:r0 + 8, c0:c0 + 128] = ag(a)[m // 14, m % 14].astype(f32)
+        for m, (r, c) in enumerate(tiles[a]):
+            d, p = place(a, m)
+            c_s[8 * r:8 * r + 8, 128 * c:128 * c + 128] = ag_s[d, p].astype(f32)
 
     def compact(ref, base, j):
         head = head_of(lax.broadcasted_iota(jnp.int32, (HD, C), 1) + C * j)
@@ -188,27 +216,27 @@
             dd(i, k).wait_send()
 
     def link(i, n):
-        slot, q = i % SLOTS, i % LAG
+        sl, q = i % SLOTS, i % LAG
         if n < 2:
-            return remote(r1_s.at[slot, 2 * n + 1 - px, :, 0:128], ra_s.at[q, n], ln_send.at[q, n], ln_recv.at[q, n], xnb)
+            return remote(r1_s.at[sl, 2 * n + 1 - px, :, 0:128], ra_s.at[q, n], ln_send.at[q, n], ln_recv.at[q, n], xnb)
         if n < 4:
-            return remote(r1_s.at[slot, 2 * (1 - py) + n - 2, :, 128:256], rb_s.at[q, n - 2], ln_send.at[q, n], ln_recv.at[q, n], ynb)
+            return remote(r1_s.at[sl, 2 * (1 - py) + n - 2, :, 128:256], rb_s.at[q, n - 2], ln_send.at[q, n], ln_recv.at[q, n], ynb)
         if n == 4:
-            return remote(r1_s.at[slot, 2 * (1 - py) + px, :, 0:128], ra2_s.at[q], ln_send.at[q, n], ln_recv.at[q, n], ynb)
-        return remote(r1_s.at[slot, 2 * py + 1 - px, :, 128:256], rb2_s.at[q], ln_send.at[q, n], ln_recv.at[q, n], xnb)
+            return remote(r1_s.at[sl, 2 * (1 - py) + px, :, 0:128], ra2_s.at[q], ln_send.at[q, n], ln_recv.at[q, n], ynb)
+        return remote(r1_s.at[sl, 2 * py + 1 - px, :, 128:256], rb2_s.at[q], ln_send.at[q, n], ln_recv.at[q, n], xnb)
 
     def first_hop(i):
         for n in (0, 2, 1, 3):
             link(i, n).start()
 
     def second_hop(i):
-        slot, q = i % SLOTS, i % LAG
+        sl, q = i % SLOTS, i % LAG
         for n in range(2):
             link(i, n).wait_recv()
-            r1_s[slot, 2 * n + px, :, 0:128] = r1_s[slot, 2 * n + px, :, 0:128] + ra_s[q, n]
+            r1_s[sl, 2 * n + px, :, 0:128] = r1_s[sl, 2 * n + px, :, 0:128] + ra_s[q, n]
         for n in range(2):
             link(i, n + 2).wait_recv()
-            r1_s[slot, 2 * py + n, :, 128:256] = r1_s[slot, 2 * py + n, :, 128:256] + rb_s[q, n]
+            r1_s[sl, 2 * py + n, :, 128:256] = r1_s[sl, 2 * py + n, :, 128:256] + rb_s[q, n]
         link(i, 4).start()
         link(i, 5).start()
 
@@ -217,16 +245,16 @@
         return pltpu.make_async_copy(ost_s.at[i % 2], dst, osem.at[i % 2])
 
     def last_sum(i):
-        slot, q = i % SLOTS, i % LAG
+        sl, q = i % SLOTS, i % LAG
 
         @pl.when(i >= 2)
         def _():
             pltpu.make_async_copy(ost_s.at[i % 2], dwq.at[:, 0:C], osem.at[i % 2]).wait()
 
         link(i, 4).wait_recv()
-        ost_s[i % 2, :, 0:128] = r1_s[slot, 2 * py + px, :, 0:128] + ra2_s[q]
+        ost_s[i % 2, :, 0:128] = r1_s[sl, 2 * py + px, :, 0:128] + ra2_s[q]
         link(i, 5).wait_recv()
-        ost_s[i % 2, :, 128:256] = r1_s[slot, 2 * py + px, :, 128:256] + rb2_s[q]
+        ost_s[i % 2, :, 128:256] = r1_s[sl, 2 * py + px, :, 128:256] + rb2_s[q]
         for n in range(6):
             link(i, n).wait_send()
 
@@ -256,66 +284,79 @@
 
     @pl.loop(0, NT_)
     def _(t):
-        x_in(t).wait()
-
-        @pl.when(t + 1 < NT_)
-        def _():
-            x_in(t + 1).start()
-
+        x_first(t).wait()
         for g in range(R // G):
-            x_hat, _ = normalise(tile_s[t % 2, G * g:G * g + G, :].astype(f32))
-            u_s[pl.ds(pl.multiple_of(t * R + G * g, G), G), :] = (x_hat * gamma + beta).astype(bf16)
+            r = pl.ds(pl.multiple_of(t * R + G * g, G), G)
+            x_hat, _ = normalise(qkv_s[0, r, :].astype(f32))
+            u_s[r, :] = (x_hat * gamma + beta).astype(bf16)
 
     dy_all.start()
-    wo_all.start()
-
-    def project(n, which, keep):
+
+    def project(n, which, j, keep=False):
         w_in(n).wait()
 
         @pl.when(n + 2 < 3 * NJ)
         def _():
             w_in(n + 2).start()
 
-        j = n % NJ
-        out = dot_nt(u_s[...], tile_s[2 + n % 3]).astype(bf16)
+        out = dot_nt(u_s[...], tile_s[slot(2 + n % 3), :]).astype(bf16)
         qkv_s[which, :, cols(j)] = out
         if keep:
             feat = phi(out.astype(f32)).astype(bf16)
             o_s[:, cols(j)] = feat
-            c_s[HD:HD + 1, cols(j)] = jnp.sum(feat.astype(f32), axis=0, keepdims=True)
-
-    c_s[HD:HD + 8, :] = jnp.zeros((8, D), f32)
-
-    @pl.loop(0, NJ)
+            zz_s[0, s, :, cols(j)] = jnp.sum(feat.astype(f32), axis=0, keepdims=True)
+
+    def state(lo, hi):
+        for j in range(lo, hi):
+            p_s[BW * j:BW * j + BW, :] = dot_tn(o_s[:, BAND[j]:BAND[j] + BW], qkv_s[2, :, C * j:C * j + C])
+            compact(p_s, BW * j, j)
+
+    @pl.loop(0, 3)
     def _(n):
-        project(n, 1, True)
-
-    @pl.loop(NJ, 2 * NJ)
+        project(n, 1, n, True)
+
+    @pl.loop(3, 5)
     def _(n):
-        project(n, 2, False)
-
-    for j in range(NJ):
-        p_s[BW * j:BW * j + BW, :] = dot_tn(o_s[:, BAND[j]:BAND[j] + BW], qkv_s[2, :, C * j:C * j + C])
-        compact(p_s, BW * j, j)
+        project(n, 2, n - 3)
+
+    state(0, 2)
     pl.semaphore_wait(barrier, 7)
     ar_start(0)
 
-    @pl.loop(2 * NJ, 3 * NJ - 2)
+    @pl.loop(5, 7)
     def _(n):
-        project(n, 0, False)
+        project(n, 1, n - 2, True)
+
+    z_start(0)
+
+    @pl.loop(7, 10)
+    def _(n):
+        project(n, 2, n - 5)
 
     ar_mid(0)
-    @pl.loop(3 * NJ - 2, 3 * NJ)
+    state(2, 5)
+    ar_start(1)
+
+    @pl.loop(10, 13)
     def _(n):
-        project(n, 0, False)
-
+        project(n, 0, n - 10)
+
+    ar_mid(1)
+
+    @pl.loop(13, 15)
+    def _(n):
+        project(n, 0, n - 10)
+
+    wo_all.start()
     bd_s[...] = jnp.zeros((D, D), bf16)
     for j in range(NJ):
         hr = head_of(lax.broadcasted_iota(jnp.int32, (C, BW), 0) + C * j)
         hc = head_of(lax.broadcasted_iota(jnp.int32, (C, BW), 1) + BAND[j])
         on_s[j] = jnp.where(hr == hc, 1.0, 0.0).astype(bf16)
 
+    z_end(0)
     ar_end(0)
+    ar_end(1)
     expand()
     for j in range(NJ):
         z = c_s[HD:HD + 1, BAND[j]:BAND[j] + BW]
@@ -332,6 +373,22 @@
             num, den = num_den(j)
             o_s[rows(t), C * j:C * j + C] = (num / den).astype(bf16)
 
+    def y_tile(t):
+        x_in(t).wait()
+
+        @pl.when(t + 1 < NT_)
+        def _():
+            x_in(t + 1).start()
+
+        @pl.when(t >= 2)
+        def _():
+            tile_out(y, t - 2).wait()
+
+        sum_ = tile_s[slot(t % 2), :].astype(f32) + dot_nn(o_s[rows(t), :], wo_s[...])
+        tile_s[slot(4 + t % 2), :] = sum_.astype(bf16)
+        tile_out(y, t).start()
+
+    x_in(0).start()
     dy_all.wait()
     wo_all.wait()
 
@@ -349,6 +406,7 @@
         def _():
             first_hop((i - 1) // 2)
 
+    y_tile(0)
     chip_sum(NJ - 1)
     second_hop(0)
     first_hop(2)
@@ -390,8 +448,9 @@
 
     for j in range(NJ):
         compact(p_s, BW * j, j)
-    c_s[HD:HD + 1, :] = -gb_s[0, 0:1, :]
-    ar_start(1)
+    zz_s[1, s] = -gb_s[0, 0:1, :]
+    ar_start(2)
+    z_start(1)
     wt_hi.start()
 
     def weight_chunk(i):
@@ -418,11 +477,17 @@
 
         @pl.when(i == NJ + 2)
         def _():
-            ar_mid(1)
-
+            ar_mid(2)
+
+
+    @pl.loop(1, 3)
+    def _(t):
+        y_tile(t)
+
+    z_end(1)
+    ar_end(2)
     chip_sum(2 * NJ - 1)
-
-    ar_end(1)
+    pump(NJ + 2, NJ, NCH)
     expand()
 
     @pl.loop(0, NT_)
@@ -437,61 +502,50 @@
             qkv_s[1, rows(t), cj] = (d_f * slope(raw)).astype(bf16)
             qkv_s[2, rows(t), cj] = dot_nn(f_s[:, band], bd_s[band, cj]).astype(bf16)
 
-        @pl.when(t % 3 == 1)
-        def _():
-            pump(NJ + 2 + t // 3, NJ, NCH)
-
-    x_in(0).start()
-    weight_chunk(2 * NJ)
-    to_mate(2 * NJ)
-
-    @pl.loop(0, NT_)
+        @pl.when((t == 3) | (t == 7))
+        def _():
+            pump(NJ + 3 + t // 7, NJ, NCH)
+
+    @pl.loop(3, NT_)
     def _(t):
-        @pl.when(t % 2 == 0)
-        def _():
-            i = 2 * NJ + 1 + t // 2
+        @pl.when(t % 2 == 1)
+        def _():
+            i = 2 * NJ + (t - 3) // 2
             weight_chunk(i)
-            chip_sum(i - 1)
+
+            @pl.when(i > 2 * NJ)
+            def _():
+                chip_sum(i - 1)
+
             to_mate(i)
-            pump(i - 1, NJ, NCH)
-
-        x_in(t).wait()
-
-        @pl.when(t + 1 < NT_)
-        def _():
-            x_in(t + 1).start()
-
-        @pl.when(t >= 2)
-        def _():
-            tile_out(y, t - 2).wait()
-
-        tile_s[4 + t % 2] = (tile_s[t % 2].astype(f32) + dot_nn(o_s[rows(t), :], wo_s[...])).astype(bf16)
-        tile_out(y, t).start()
+
+            @pl.when(i == 2 * NJ + 1)
+            def _():
+                pump(2 * NJ, NJ, NCH)
+
+        y_tile(t)
 
     wt_lo.start()
     tile_out(y, NT_ - 2).wait()
     tile_out(y, NT_ - 1).wait()
-
     gb_s[...] = jnp.zeros((2, 8, D), f32)
     x_in(0).start()
     dy_in(0).start()
 
     @pl.loop(0, NT_)
     def _(t):
-        @pl.when(t < NJ)
-        def _():
-            weight_chunk(3 * NJ + t)
-
-        @pl.when(t <= NJ)
-        def _():
-            chip_sum(3 * NJ - 1 + t)
-
-        @pl.when(t < NJ)
-        def _():
-            to_mate(3 * NJ + t)
-
-        pump(3 * NJ - 1 + t, NJ, NCH)
-
+        @pl.when(t < 7)
+        def _():
+            weight_chunk(2 * NJ + 3 + t)
+
+        @pl.when(t < 7)
+        def _():
+            chip_sum(2 * NJ + 2 + t)
+            to_mate(2 * NJ + 3 + t)
+
+        @pl.when(t < NT_ - 1)
+        def _():
+            pump(2 * NJ + 1 + t + t // 4, NJ, NCH)
         @pl.when(t == 0)
         def _():
             wt_lo.wait()
@@ -519,9 +573,17 @@
                             + dot_nn(qkv_s[1, rows(t), cut:D], g_s[0:D - cut, cj])
                             + dot_nn(qkv_s[2, rows(t), :], g_s[D - cut:2 * D - cut, cj]))
 
+        @pl.when(t == 6)
+        def _():
+            chip_sum(NCH - 1)
+
+        @pl.when((t == 3) | (t >= 6))
+        def _():
+            pump(2 * NJ + 5 + 4 * (t // 6) + t // 7, NJ, NCH)
+
         for g in range(R // G):
             gs = slice(G * g, G * g + G)
-            x_hat, inv = normalise(tile_s[t % 2, gs, :].astype(f32))
+            x_hat, inv = normalise(tile_s[pl.ds(pl.multiple_of((t % 2) * R + G * g, G), G), :].astype(f32))
             du = acc_s[gs, :]
             dux = du * x_hat
             gb_s[0] = gb_s[0] + sum(dux[8 * q:8 * q + 8, :] for q in range(G // 8))
@@ -529,7 +591,7 @@
             e = du * gamma
             m1 = jnp.mean(e, axis=-1, keepdims=True)
             m2 = jnp.mean(e * x_hat, axis=-1, keepdims=True)
-            tile_s[4 + t % 2, gs, :] = (tile_s[2 + t % 2, gs, :].astype(f32) + inv * (e - m1 - x_hat * m2)).astype(bf16)
+            tile_s[pl.ds(pl.multiple_of((4 + t % 2) * R + G * g, G), G), :] = (tile_s[pl.ds(pl.multiple_of((2 + t % 2) * R + G * g, G), G), :].astype(f32) + inv * (e - m1 - x_hat * m2)).astype(bf16)
 
         tile_out(dx, t).start()
 
@@ -541,7 +603,7 @@
     for k in range(1, 8):
         gb_copy(k).start()
 
-    @pl.loop(NCH + 2, NCH + 4)
+    @pl.loop(NCH + 1, NCH + 4)
     def _(m):
         pump(m, NJ, NCH)
 
@@ -573,17 +635,17 @@
         pltpu.VMEM((D, D), bf16),
         pltpu.VMEM((NJ, C, BW), bf16),
         pltpu.VMEM((NJ, C, BW), bf16),
-        pltpu.VMEM((6, R, D), bf16),
+        pltpu.VMEM((6 * R, D), bf16),
         pltpu.VMEM((R, D), bf16),
         pltpu.VMEM((R, D), f32),
         pltpu.VMEM((R, D), f32),
         pltpu.VMEM((R, D), bf16),
         pltpu.VMEM((R, D), bf16),
         pltpu.VMEM((HD + 8, D), f32),
-        pltpu.VMEM((8, 14, 8, 128), f32),
-        pltpu.VMEM((8, 14, 8, 128), f32),
-        pltpu.VMEM((8, 14, 8, 128), bf16),
-        pltpu.VMEM((8, 14, 8, 128), f32),
+        pltpu.VMEM((2, 8, 1, D), f32),
+        pltpu.VMEM((8, 13, 8, 128), f32),
+        pltpu.VMEM((8, 13, 8, 128), f32),
+        pltpu.VMEM((8, 13, 8, 128), bf16),
         pltpu.VMEM((8, 2, D), f32),
         pltpu.VMEM((2, 8, D), f32),
         pltpu.VMEM((2 * D, C), f32),
@@ -593,8 +655,8 @@
         pltpu.VMEM((LAG, PIECE, 128), f32),
         pltpu.VMEM((LAG, PIECE, 128), f32),
         pltpu.VMEM((2, PIECE, C), f32),
-        dma((2,)), dma((2,)), dma((2,)), dma((3,)), dma((3,)), dma((2,)),
-        dma((2, 2, 8)), dma((2, 2, 8)), dma((8,)), dma((8,)),
+        dma((NT_,)), dma((2,)), dma((2,)), dma((2,)), dma((3,)), dma((3,)), dma((2,)),
+        dma((2, 8)), dma((2, 8)), dma((3, 2, 8)), dma((3, 2, 8)), dma((8,)), dma((8,)),
         dma((2, 4)), dma((2, 4)), dma((LAG, 6)), dma((LAG, 6)),
     ]
     y, dx, dwq, dwo, dgam, dbet = pl.pallas_call(

time: 204 us -> 192 us (0.941)
  Pallas kernels: 187 us -> 176 us
    pallas_call x1, Pallas kernels: 187 us -> 176 us  [local_block(): pl.pallas_call(block, name='block', out_shape=(jax.ShapeDtypeStruct((T, D...]
where the time goes in v3:
time: 192 us
  Pallas kernels  176 us (92%)
  local copies, waits for them, and re-layouts  15.6 us (8%)
    pallas_call x1, Pallas kernels, local_block(): pl.pallas_call(block, name='block', out_shape=(jax.ShapeDtypeStruct((T, D...  176 us
    unnamed x15, local copies, waits for them, and re-layouts  9.8 us
    reshape x1, local copies, waits for them, and re-layouts, local_block(): return (y, dx, dwq.reshape(PIECE, 3, NH, HD), dwo, dgam, dbet)  5.83 us

profile of v3, /device:TPU:0, one launch (start us, length us, event | category | flops | bytes accessed | tf_op | source)
XLA Modules:
  0.0 192.0 jit_solution(3532606884186933657)
XLA Ops:
  0.6 175.7 %block.1 = (bf16[2048,1280]{1,0:T(8,128)(2,1)}, bf16[2048,1280]{1,0:T(8,128)(2,1)}, f32[160,3840]{1,0:T(8,128)}, f32[160,1280]{1,0:T(8,128)}, f32[1280]{0:T(1024)}, /*index=5*/f32[1280]{0:T(1024)}) custom-call(bf16[2048,1280]{1,0:T(8,128)(2,1)} %x.1, bf16[2048,1280]{1,0:T(8,128)(2,1)} %dy.1, bf16[3840,1280]{1,0:T(8,128)(2,1)} %bitcast.3, ...), custom_call_target="tpu_custom_call" | custom-call | tf_op jit(solution)/shard_map/block/pallas_call | solution.py:662
  176.4 0.0 slice-start
  176.4 5.8 %reshape.19 = f32[160,3,16,80]{3,2,1,0:T(8,128)} reshape(f32[160,3840]{1,0:T(8,128)} %get-tuple-element.14) | data formatting | bytes 4915200 | tf_op jit(solution)/shard_map/reshape | solution.py:673
  182.2 0.0 slice-start.1
  182.2 5.3 %copy.17 = bf16[2048,1280]{1,0:T(8,128)(2,1)} copy(bf16[2048,1280]{1,0:T(8,128)(2,1)} %get-tuple-element.24) | data formatting | bytes 10485760
  187.5 0.0 slice-done
  187.5 0.0 slice-done.1
  187.5 0.0 copy-start
  187.5 0.0 copy-start.2
  187.6 0.0 copy-start.1
  187.6 2.4 %copy.18 = bf16[2048,1280]{1,0:T(8,128)(2,1)} copy(bf16[2048,1280]{1,0:T(8,128)(2,1)S(1)} %bitcast.5) | data formatting | bytes 10485760
  189.9 0.0 copy-done
  189.9 0.9 copy.19
  190.8 0.0 copy-done.2
  190.8 0.6 copy.20
  191.4 0.0 copy-done.1
  191.4 0.6 copy.21
  (1 shorter events, 0.0 us)
Async XLA Ops:
  176.4 11.2 %slice-start = ((s8[5242880]{0:T(1024)(128)(4,1)}), s8[1048576]{0:T(1024)(128)(4,1)S(1)}, s32[]{:S(2)}) async-start(s8[5242880]{0:T(1024)(128)(4,1)} %bitcast.4), calls=%async_computation | async-start | bytes 2097152
  182.2 5.3 %slice-start.1 = ((s8[5242880]{0:T(1024)(128)(4,1)}), s8[4194304]{0:T(1024)(128)(4,1)S(1)}, s32[]{:S(2)}) async-start(s8[5242880]{0:T(1024)(128)(4,1)} %bitcast.4), calls=%async_computation.1 | async-start | bytes 8388608
  187.5 2.4 %copy-start = (f32[160,1280]{1,0:T(8,128)S(1)}, f32[160,1280]{1,0:T(8,128)}, u32[]{:S(2)}) copy-start(f32[160,1280]{1,0:T(8,128)} %get-tuple-element.27) | copy-start | bytes 2457604
  187.5 3.3 %copy-start.2 = (f32[1280]{0:T(1024)S(1)}, f32[1280]{0:T(1024)}, u32[]{:S(2)}) copy-start(f32[1280]{0:T(1024)} %get-tuple-element.28) | copy-start | bytes 15364
  187.6 3.9 %copy-start.1 = (f32[1280]{0:T(1024)S(1)}, f32[1280]{0:T(1024)}, u32[]{:S(2)}) copy-start(f32[1280]{0:T(1024)} %get-tuple-element.29) | copy-start | bytes 15364

commit v4 on v3

--- a/solution.py
+++ b/solution.py
@@ -545,7 +545,7 @@
 
         @pl.when(t < NT_ - 1)
         def _():
-            pump(2 * NJ + 1 + t + t // 4, NJ, NCH)
+            pump(2 * NJ + 1 + t + (t + 6) // 8, NJ, NCH)
         @pl.when(t == 0)
         def _():
             wt_lo.wait()
@@ -577,9 +577,9 @@
         def _():
             chip_sum(NCH - 1)
 
-        @pl.when((t == 3) | (t >= 6))
-        def _():
-            pump(2 * NJ + 5 + 4 * (t // 6) + t // 7, NJ, NCH)
+        @pl.when((t == 1) | (t >= 6))
+        def _():
+            pump(2 * NJ + 2 + t + t // 6, NJ, NCH)
 
         for g in range(R // G):
             gs = slice(G * g, G * g + G)

time: 192 us -> 191 us (level)
  Pallas kernels: 176 us -> 174 us
where the time goes in v4:
time: 191 us; the launch traced here: 190 us
  Pallas kernels  174 us (91%)
  local copies, waits for them, and re-layouts  15.6 us (8%)
    pallas_call x1, Pallas kernels, local_block(): pl.pallas_call(block, name='block', out_shape=(jax.ShapeDtypeStruct((T, D...  174 us
    unnamed x15, local copies, waits for them, and re-layouts  9.8 us
    reshape x1, local copies, waits for them, and re-layouts, local_block(): return (y, dx, dwq.reshape(PIECE, 3, NH, HD), dwo, dgam, dbet)  5.83 us

profile of v4, /device:TPU:0, one launch (start us, length us, event | category | flops | bytes accessed | tf_op | source)
XLA Modules:
  0.0 190.2 jit_solution(13512514564725979137)
XLA Ops:
  0.6 173.9 %block.1 = (bf16[2048,1280]{1,0:T(8,128)(2,1)}, bf16[2048,1280]{1,0:T(8,128)(2,1)}, f32[160,3840]{1,0:T(8,128)}, f32[160,1280]{1,0:T(8,128)}, f32[1280]{0:T(1024)}, /*index=5*/f32[1280]{0:T(1024)}) custom-call(bf16[2048,1280]{1,0:T(8,128)(2,1)} %x.1, bf16[2048,1280]{1,0:T(8,128)(2,1)} %dy.1, bf16[3840,1280]{1,0:T(8,128)(2,1)} %bitcast.3, ...), custom_call_target="tpu_custom_call" | custom-call | tf_op jit(solution)/shard_map/block/pallas_call | solution.py:662
  174.6 0.0 slice-start
  174.6 5.8 %reshape.19 = f32[160,3,16,80]{3,2,1,0:T(8,128)} reshape(f32[160,3840]{1,0:T(8,128)} %get-tuple-element.14) | data formatting | bytes 4915200 | tf_op jit(solution)/shard_map/reshape | solution.py:673
  180.4 0.0 slice-start.1
  180.4 5.3 %copy.17 = bf16[2048,1280]{1,0:T(8,128)(2,1)} copy(bf16[2048,1280]{1,0:T(8,128)(2,1)} %get-tuple-element.24) | data formatting | bytes 10485760
  185.7 0.0 slice-done
  185.8 0.0 slice-done.1
  185.8 0.0 copy-start
  185.8 0.0 copy-start.2
  185.8 0.0 copy-start.1
  185.8 2.4 %copy.18 = bf16[2048,1280]{1,0:T(8,128)(2,1)} copy(bf16[2048,1280]{1,0:T(8,128)(2,1)S(1)} %bitcast.5) | data formatting | bytes 10485760
  188.1 0.0 copy-done
  188.1 0.9 copy.19
  189.0 0.0 copy-done.2
  189.0 0.6 copy.20
  189.6 0.0 copy-done.1
  189.6 0.6 copy.21
  (1 shorter events, 0.0 us)
Async XLA Ops:
  174.6 11.2 %slice-start = ((s8[5242880]{0:T(1024)(128)(4,1)}), s8[1048576]{0:T(1024)(128)(4,1)S(1)}, s32[]{:S(2)}) async-start(s8[5242880]{0:T(1024)(128)(4,1)} %bitcast.4), calls=%async_computation | async-start | bytes 2097152
  180.4 5.3 %slice-start.1 = ((s8[5242880]{0:T(1024)(128)(4,1)}), s8[4194304]{0:T(1024)(128)(4,1)S(1)}, s32[]{:S(2)}) async-start(s8[5242880]{0:T(1024)(128)(4,1)} %bitcast.4), calls=%async_computation.1 | async-start | bytes 8388608
  185.8 2.4 %copy-start = (f32[160,1280]{1,0:T(8,128)S(1)}, f32[160,1280]{1,0:T(8,128)}, u32[]{:S(2)}) copy-start(f32[160,1280]{1,0:T(8,128)} %get-tuple-element.27) | copy-start | bytes 2457604
  185.8 3.3 %copy-start.2 = (f32[1280]{0:T(1024)S(1)}, f32[1280]{0:T(1024)}, u32[]{:S(2)}) copy-start(f32[1280]{0:T(1024)} %get-tuple-element.28) | copy-start | bytes 15364
  185.8 3.9 %copy-start.1 = (f32[1280]{0:T(1024)S(1)}, f32[1280]{0:T(1024)}, u32[]{:S(2)}) copy-start(f32[1280]{0:T(1024)} %get-tuple-element.29) | copy-start | bytes 15364

commit v5 on v4

--- a/solution.py
+++ b/solution.py
@@ -519,9 +519,9 @@
 
             to_mate(i)
 
-            @pl.when(i == 2 * NJ + 1)
+            @pl.when(i > 2 * NJ)
             def _():
-                pump(2 * NJ, NJ, NCH)
+                pump(i - 1, NJ, NCH)
 
         y_tile(t)
 
@@ -545,7 +545,7 @@
 
         @pl.when(t < NT_ - 1)
         def _():
-            pump(2 * NJ + 1 + t + (t + 6) // 8, NJ, NCH)
+            pump(2 * NJ + 2 + t, NJ, NCH)
         @pl.when(t == 0)
         def _():
             wt_lo.wait()
@@ -577,7 +577,7 @@
         def _():
             chip_sum(NCH - 1)
 
-        @pl.when((t == 1) | (t >= 6))
+        @pl.when(t >= 6)
         def _():
             pump(2 * NJ + 2 + t + t // 6, NJ, NCH)
 

time: 191 us -> 192 us (level)
  Pallas kernels: 174 us -> 176 us
where the time goes in v5:
time: 192 us
  Pallas kernels  176 us (92%)
  local copies, waits for them, and re-layouts  15.6 us (8%)
    pallas_call x1, Pallas kernels, local_block(): pl.pallas_call(block, name='block', out_shape=(jax.ShapeDtypeStruct((T, D...  176 us
    unnamed x15, local copies, waits for them, and re-layouts  9.8 us
    reshape x1, local copies, waits for them, and re-layouts, local_block(): return (y, dx, dwq.reshape(PIECE, 3, NH, HD), dwo, dgam, dbet)  5.83 us

profile of v5, /device:TPU:0, one launch (start us, length us, event | category | flops | bytes accessed | tf_op | source)
XLA Modules:
  0.0 191.8 jit_solution(10863495294918137284)
XLA Ops:
  0.6 175.5 %block.1 = (bf16[2048,1280]{1,0:T(8,128)(2,1)}, bf16[2048,1280]{1,0:T(8,128)(2,1)}, f32[160,3840]{1,0:T(8,128)}, f32[160,1280]{1,0:T(8,128)}, f32[1280]{0:T(1024)}, /*index=5*/f32[1280]{0:T(1024)}) custom-call(bf16[2048,1280]{1,0:T(8,128)(2,1)} %x.1, bf16[2048,1280]{1,0:T(8,128)(2,1)} %dy.1, bf16[3840,1280]{1,0:T(8,128)(2,1)} %bitcast.3, ...), custom_call_target="tpu_custom_call" | custom-call | tf_op jit(solution)/shard_map/block/pallas_call | solution.py:662
  176.2 0.0 slice-start
  176.2 5.8 %reshape.19 = f32[160,3,16,80]{3,2,1,0:T(8,128)} reshape(f32[160,3840]{1,0:T(8,128)} %get-tuple-element.14) | data formatting | bytes 4915200 | tf_op jit(solution)/shard_map/reshape | solution.py:673
  182.0 0.0 slice-start.1
  182.0 5.3 %copy.17 = bf16[2048,1280]{1,0:T(8,128)(2,1)} copy(bf16[2048,1280]{1,0:T(8,128)(2,1)} %get-tuple-element.24) | data formatting | bytes 10485760
  187.3 0.0 slice-done
  187.4 0.0 slice-done.1
  187.4 0.0 copy-start
  187.4 0.0 copy-start.2
  187.4 0.0 copy-start.1
  187.4 2.4 %copy.18 = bf16[2048,1280]{1,0:T(8,128)(2,1)} copy(bf16[2048,1280]{1,0:T(8,128)(2,1)S(1)} %bitcast.5) | data formatting | bytes 10485760
  189.7 0.0 copy-done
  189.7 0.9 copy.19
  190.6 0.0 copy-done.2
  190.6 0.6 copy.20
  191.2 0.0 copy-done.1
  191.2 0.6 copy.21
  (1 shorter events, 0.0 us)
Async XLA Ops:
  176.2 11.2 %slice-start = ((s8[5242880]{0:T(1024)(128)(4,1)}), s8[1048576]{0:T(1024)(128)(4,1)S(1)}, s32[]{:S(2)}) async-start(s8[5242880]{0:T(1024)(128)(4,1)} %bitcast.4), calls=%async_computation | async-start | bytes 2097152
  182.0 5.3 %slice-start.1 = ((s8[5242880]{0:T(1024)(128)(4,1)}), s8[4194304]{0:T(1024)(128)(4,1)S(1)}, s32[]{:S(2)}) async-start(s8[5242880]{0:T(1024)(128)(4,1)} %bitcast.4), calls=%async_computation.1 | async-start | bytes 8388608
  187.4 2.4 %copy-start = (f32[160,1280]{1,0:T(8,128)S(1)}, f32[160,1280]{1,0:T(8,128)}, u32[]{:S(2)}) copy-start(f32[160,1280]{1,0:T(8,128)} %get-tuple-element.27) | copy-start | bytes 2457604
  187.4 3.3 %copy-start.2 = (f32[1280]{0:T(1024)S(1)}, f32[1280]{0:T(1024)}, u32[]{:S(2)}) copy-start(f32[1280]{0:T(1024)} %get-tuple-element.28) | copy-start | bytes 15364
  187.4 3.9 %copy-start.1 = (f32[1280]{0:T(1024)S(1)}, f32[1280]{0:T(1024)}, u32[]{:S(2)}) copy-start(f32[1280]{0:T(1024)} %get-tuple-element.29) | copy-start | bytes 15364
